TPU v7x, 32 devices: a whole 2x2x4 slice. The times are simulated.
32 devices in a mesh: img: 2 (over x), ga: 4 (over y, core), band: 4 (over z).
Axes of the slice: x: 2, y: 2, z: 4, core: 2. Of those that a mesh axis runs over, the one named last changes fastest.
Arguments:
- orbitals: bfloat16 [1536, 12288], P(('img', 'band'), 'ga'), parts along dimension 0, as said below
- kernel: float32 [12288], P('ga'), may hold values from 0.3 to 3
- block_vectors: bfloat16 [512, 12288], P(('img', 'band'), 'ga'), parts along dimension 0
Outputs:
- ace_vectors: bfloat16 [1536, 12288], P(('img', 'band'), 'ga'), parts along dimension 0
- exchange_block: bfloat16 [512, 12288], P(('img', 'band'), 'ga'), parts along dimension 0
There are 2 independent parts, one for each index of `img`. A program takes and returns all parts, laid end to end along the dimension named above; an argument that names none is the same for every part. Nothing has to cross between parts.
Inputs may be any that keep to these rules, and one draw needn't show every extreme that they name: `orbitals`: the bands of one image are linearly independent, and the block lies largely in their span.
All inputs are finite; a program needn't handle non-finite values.
Results may differ from a plain program's by a relative error of at most 0.02.
Values may be sent and summed in bfloat16 or wider, within the bound.
A program may use at most 64 MiB of HBM per device.

v0:
```python
import functools

import jax
import jax.numpy as jnp
from jax import lax
from jax.experimental import pallas as pl
from jax.experimental.pallas import tpu as pltpu
from jax.sharding import PartitionSpec as P

MESH = pl.DeviceIdType.MESH
F32 = jnp.float32
BF16 = jnp.bfloat16
TILE = 128


def send(src, dst, send_sem, recv_sem, where):
    copy = pltpu.make_async_remote_copy(
        src_ref=src, dst_ref=dst, send_sem=send_sem, recv_sem=recv_sem,
        device_id=where, device_id_type=MESH,
    )
    copy.start()
    return copy


def greet(places):
    barrier = pltpu.get_barrier_semaphore()
    for place in places:
        pl.semaphore_signal(barrier, inc=1, device_id=place, device_id_type=MESH)
    pl.semaphore_wait(barrier, len(places))


def dot(a, b, dims):
    return lax.dot_general(a, b, (dims, ((), ())), preferred_element_type=F32)


class Place:
    def __init__(self, bands, groups):
        self.bands = bands
        self.me = lax.axis_index("band")
        ga = lax.axis_index("ga")
        self.core = lax.rem(ga, 2)
        self.row = lax.rem(ga // 2, 2)
        self.partner = {"ga": ga + 1 - 2 * self.core}
        self.across = {"ga": ga + 2 - 4 * self.row}
        self.peer = [lax.rem(self.me + d, bands) for d in range(bands)]
        self.far = sorted(range(1, bands), key=lambda d: -min(d, bands - d))
        self.near = self.far[::-1]
        self.bits = []
        stride = 4
        while stride < groups:
            self.bits.append({"ga": ga + stride * (1 - 2 * lax.rem(ga // stride, 2))})
            stride *= 2

    def band(self, d):
        return {"band": self.peer[d]}

    def everyone(self):
        return [self.band(d) for d in range(1, self.bands)] + [self.partner, self.across] + self.bits


def span(index, size, offset=0):
    return pl.ds(pl.multiple_of(offset + index * size, 16), size)


def reduce_scratch(rows, bands, levels):
    h1, h2 = rows // 2, rows // 4
    h3 = h2 // bands
    dma = pltpu.SemaphoreType.DMA
    shapes = [
        ((rows, TILE), F32), ((rows, TILE), BF16), ((h1, TILE), BF16),
        ((h1, TILE), F32), ((h1, TILE), BF16), ((h2, TILE), BF16),
        ((h2, TILE), F32), ((h2, TILE), BF16), ((bands, h3, TILE), BF16),
        ((levels, h3, TILE), BF16), ((levels, h3, TILE), BF16), ((rows, TILE), BF16),
    ]
    return [pltpu.VMEM(*shape) for shape in shapes] + [
        dma((4,)), dma((bands,)), dma((bands,)), dma((levels,)), dma((levels,)),
        dma((bands,)), dma((bands,)), dma((bands,)), dma((bands,)),
        dma((2 * bands,)), dma((2 * bands,)),
    ]


def reduce_stages(at, scratch):
    (p32, p16, rx1, a32, a16, rx2, b32, b16, rx3, out_x, rx_x, allg,
     one, z_s, z_r, x_s, x_r, g_s, g_r, y_s, y_r, f_s, f_r) = scratch
    h1, h2 = rx1.shape[0], rx2.shape[0]
    h3 = h2 // at.bands
    copy = send(p16.at[span(1 - at.core, h1)], rx1, one.at[0], one.at[1], at.partner)
    yield
    copy.wait()
    a32[...] = p32[span(at.core, h1), :] + rx1[...].astype(F32)
    a16[...] = a32[...].astype(BF16)
    copy = send(a16.at[span(1 - at.row, h2)], rx2, one.at[2], one.at[3], at.across)
    yield
    copy.wait()
    b32[...] = a32[span(at.row, h2), :] + rx2[...].astype(F32)
    b16[...] = b32[...].astype(BF16)
    copies = [send(b16.at[span(at.peer[d], h3)], rx3.at[d], z_s.at[d], z_r.at[d], at.band(d))
              for d in at.far]
    yield
    for copy in copies:
        copy.wait()
    total = b32[span(at.me, h3), :]
    for d in range(1, at.bands):
        total = total + rx3[d].astype(F32)
    for i, place in enumerate(at.bits):
        out_x[i] = total.astype(BF16)
        send(out_x.at[i], rx_x.at[i], x_s.at[i], x_r.at[i], place).wait()
        total = out_x[i].astype(F32) + rx_x[i].astype(F32)

    def piece(d, row):
        source = lax.rem(at.me + at.bands - d, at.bands)
        return allg.at[span(source, h3, at.core * h1 + row * h2)]

    allg[span(at.me, h3, at.core * h1 + at.row * h2), :] = total.astype(BF16)
    own = piece(0, at.row)
    gathers = {d: send(own, own, g_s.at[d], g_r.at[d], at.band(d)) for d in at.far}
    sides = {0: send(own, own, y_s.at[0], y_r.at[0], at.across)}
    lasts = [send(own, own, f_s.at[0], f_r.at[0], at.partner)]
    yield
    for d in at.near:
        gathers[d].wait()
        there = piece(d, at.row)
        sides[d] = send(there, there, y_s.at[d], y_r.at[d], at.across)
        lasts.append(send(there, there, f_s.at[d], f_r.at[d], at.partner))
    yield
    for d in [0] + at.near:
        sides[d].wait()
        there = piece(d, 1 - at.row)
        e = at.bands + d
        lasts.append(send(there, there, f_s.at[e], f_r.at[e], at.partner))
    yield
    for copy in lasts:
        copy.wait()


def margin_kernel(bands, groups, orb, kern, m_out, w_out, full, loc, a_s, a_r, *scratch):
    at = Place(bands, groups)
    own = orb.shape[0]
    cols = orb.shape[1] // bands
    n = own * bands
    greet(at.everyone())

    def chunk(d):
        return pl.ds(pl.multiple_of(at.peer[d] * cols, TILE), cols)

    mine = full.at[span(at.me, own)]
    local = pltpu.make_async_copy(orb.at[:, chunk(0)], mine, loc.at[0])
    local.start()
    copies = [send(orb.at[:, chunk(d)], mine, a_s.at[d], a_r.at[d], at.band(d)) for d in at.far]
    local.wait()
    for copy in copies:
        copy.wait()
    w_out[...] = (-(full[...].astype(F32) * kern[:, chunk(0)])).astype(BF16)
    p32, p16, allg = scratch[0], scratch[1], scratch[11]
    row = 0
    for s in range(0, n, TILE):
        e = s + TILE
        product = dot(w_out[s:e, :], full[0:e, :], ((1,), (1,)))
        for c in range(0, e, TILE):
            p32[row:row + TILE, :] = product[:, c:c + TILE]
            p16[row:row + TILE, :] = product[:, c:c + TILE].astype(BF16)
            row += TILE
    if row < p32.shape[0]:
        p32[row:, :] = jnp.zeros((p32.shape[0] - row, TILE), F32)
        p16[row:, :] = jnp.zeros((p32.shape[0] - row, TILE), BF16)
    for _ in reduce_stages(at, scratch):
        pass
    m_out[...] = allg[...]


def split(a):
    high = a.astype(BF16)
    return high, (a - high.astype(F32)).astype(BF16)


def product3(a, b, dims):
    (ah, al), (bh, bl) = split(a), split(b)
    return dot(ah, bh, dims) + (dot(ah, bl, dims) + dot(al, bh, dims))


def identity(rows):
    shape = (rows, rows)
    return (lax.broadcasted_iota(jnp.int32, shape, 0)
            == lax.broadcasted_iota(jnp.int32, shape, 1)).astype(F32)


def factor_tile(d_ref, t_ref):
    G, SUB = 32, 8
    H = G // SUB
    sub = lax.broadcasted_iota(jnp.int32, (SUB, TILE), 0)

    def spread(block, i):
        return jnp.broadcast_to(block[i:i + 1, :], (SUB, TILE))

    def lane(block, c):
        return jnp.broadcast_to(block[:, c:c + 1], (SUB, TILE))

    def step(g, carry):
        start = pl.multiple_of(g * G, G)
        turned = pltpu.roll(d_ref[pl.ds(start, G), 0:TILE], lax.rem(TILE - start, TILE), 1)
        right = d_ref[pl.ds(start, G), TILE:2 * TILE]
        lefts = [turned[h * SUB:(h + 1) * SUB, :] for h in range(H)]
        rights = [right[h * SUB:(h + 1) * SUB, :] for h in range(H)]
        us, vs = [], []
        for b in range(H):
            columns = [lane(lefts[b], b * SUB + c) for c in range(SUB)]
            d = [[spread(columns[c], i) for c in range(i + 1)] for i in range(SUB)]
            below = {h: [lane(lefts[h], b * SUB + c) for c in range(SUB)] for h in range(b + 1, H)}
            u, v = [], []
            u_all = v_all = jnp.zeros((SUB, TILE), F32)
            for j in range(SUB):
                r = lax.rsqrt(d[j][j])
                for i in range(j + 1, SUB):
                    d[i][j] = d[i][j] * r
                for i in range(j + 1, SUB):
                    for c in range(j + 1, i + 1):
                        d[i][c] = d[i][c] - d[i][j] * d[c][j]
                p, q = spread(lefts[b], j), spread(rights[b], j)
                for t in range(j):
                    p = p - d[j][t] * u[t]
                    q = q - d[j][t] * v[t]
                u.append(p * r)
                v.append(q * r)
                u_all = jnp.where(sub == j, u[j], u_all)
                v_all = jnp.where(sub == j, v[j], v_all)
                for h in range(b + 1, H):
                    n = below[h][j]
                    for t in range(j):
                        n = n - below[h][t] * d[j][t]
                    below[h][j] = n * r
            us.append(u_all)
            vs.append(v_all)
            for h in range(b + 1, H):
                for j in range(SUB):
                    lefts[h] = lefts[h] - below[h][j] * u[j]
                    rights[h] = rights[h] - below[h][j] * v[j]
        u_all = pltpu.roll(jnp.concatenate(us, axis=0), start, 1)
        v_all = jnp.concatenate(vs, axis=0)
        t_ref[pl.ds(start, G), :] = v_all
        both = jnp.concatenate([u_all, v_all], axis=1)
        high = both.astype(BF16).astype(F32)
        low = both - high
        lhs = jnp.concatenate([high[:, :TILE], high[:, :TILE], low[:, :TILE]], axis=0)
        rhs = jnp.concatenate([high, low, high], axis=0)
        d_ref[...] -= dot(lhs.astype(BF16), rhs.astype(BF16), ((0,), (0,)))
        return carry

    lax.fori_loop(0, TILE // G, step, 0)


def apply_kernel(bands, groups, m_ref, w, blk, ace, exch, a, rest, d_ref, t_ref, x16, proj,
                 bfull, applied, loc, b_s, b_r, p_s, p_r, e_s, e_r, *scratch):
    at = Place(bands, groups)
    me = at.me
    own, bown = ace.shape[0], exch.shape[0]
    cols = w.shape[1]
    n, nblk = own * bands, bown * bands
    scale = 1.0 / (ace.shape[1] * groups)
    greet(at.everyone())

    def chunk(index):
        return pl.ds(pl.multiple_of(index * cols, TILE), cols)

    mine = bfull.at[span(me, bown)]
    local = pltpu.make_async_copy(blk.at[:, chunk(me)], mine, loc.at[0])
    local.start()
    blocks = [send(blk.at[:, chunk(at.peer[d])], mine, b_s.at[d], b_r.at[d], at.band(d))
              for d in at.far]
    row = 0
    for s in range(0, n, TILE):
        for c in range(0, s + TILE, TILE):
            a[s:s + TILE, c:c + TILE] = m_ref[row:row + TILE, :].astype(F32) * -scale
            row += TILE
    rest[...] = identity(n)
    x16[...] = jnp.zeros_like(x16)
    p32, p16, allg = scratch[0], scratch[1], scratch[11]

    def stages():
        local.wait()
        for copy in blocks:
            copy.wait()
        half = nblk // 2
        for h in range(2):
            product = dot(w[...], bfull[h * half:(h + 1) * half, :], ((1,), (1,)))
            p32[h * n:(h + 1) * n, :] = product
            p16[h * n:(h + 1) * n, :] = product.astype(BF16)
        yield from reduce_stages(at, scratch)

    cuts = sorted(set(range(0, n, TILE)) | set(range(0, n, own)) | {n})
    pieces = list(enumerate(zip(cuts[:-1], cuts[1:])))

    def piece(q, r0, r1, source, target):
        lo = r0 % own
        return pltpu.make_async_remote_copy(
            src_ref=proj.at[r0:r1], dst_ref=ace.at[lo:lo + r1 - r0, chunk(source)],
            send_sem=p_s.at[q], recv_sem=p_r.at[q, source],
            device_id={"band": target}, device_id_type=MESH)

    def kept(q, r0, r1):
        lo = r0 % own
        return pltpu.make_async_copy(
            proj.at[r0:r1], ace.at[lo:lo + r1 - r0, chunk(me)], p_s.at[q])

    steps = stages()
    for s in range(0, n, TILE):
        e = s + TILE
        d_ref[:, 0:TILE] = a[s:e, s:e]
        d_ref[:, TILE:] = identity(TILE)
        factor_tile(d_ref, t_ref)
        tile = t_ref[...]
        rows = product3(tile, rest[s:e, 0:e], ((1,), (0,)))
        high, low = split(rows)
        x16[s:e, 0:e] = high
        proj[s:e, :] = (dot(high, w[0:e, :], ((1,), (0,)))
                        + dot(low, w[0:e, :], ((1,), (0,)))).astype(BF16)
        for q, (r0, r1) in pieces:
            if s <= r0 < e:
                owner = r0 // own

                @pl.when(me != owner)
                def _():
                    piece(q, r0, r1, me, owner).start()

                @pl.when(me == owner)
                def _():
                    kept(q, r0, r1).start()
        if e < n:
            panel = product3(a[e:, s:e], tile, ((1,), (1,)))
            for c in range(e, n, TILE):
                a[c:, c:c + TILE] -= product3(panel[c - e:], panel[c - e:c - s], ((1,), (1,)))
            rest[e:, 0:e] -= product3(panel, rows, ((1,), (0,)))
        next(steps, None)
    for _ in steps:
        pass
    half = nblk // 2
    for h in range(2):
        coupling = dot(x16[...], allg[h * n:(h + 1) * n, :], ((1,), (0,))) * scale
        applied[h * half:(h + 1) * half, :] = (
            -dot(coupling.astype(BF16), proj[...], ((0,), (0,)))).astype(BF16)
    outs = [send(applied.at[span(at.peer[d], bown)], exch.at[:, chunk(me)],
                 e_s.at[d], e_r.at[d], at.band(d)) for d in at.far]
    outs.append(pltpu.make_async_copy(applied.at[span(me, bown)], exch.at[:, chunk(me)], loc.at[1]))
    outs[-1].start()
    for q, (r0, r1) in pieces:
        owner = r0 // own

        @pl.when(me != owner)
        def _():
            piece(q, r0, r1, me, owner).wait_send()

        @pl.when(me == owner)
        def _():
            kept(q, r0, r1).wait()
            for d in range(1, bands):
                piece(q, r0, r1, at.peer[d], at.peer[d]).wait_recv()
    for copy in outs:
        copy.wait()


def shards(orbitals, kernel, block_vectors):
    groups, bands = lax.axis_size("ga"), lax.axis_size("band")
    own, width = orbitals.shape
    bown = block_vectors.shape[0]
    cols = width // bands
    n, nblk = own * bands, bown * bands
    levels = max(groups.bit_length() - 3, 1)
    unit = 4 * bands * 16
    tiles = n // TILE
    flat = -(-(tiles * (tiles + 1) // 2 * TILE) // unit) * unit
    pieces = len(set(range(0, n, TILE)) | set(range(0, n, own)))
    vmem, hbm = pl.BlockSpec(memory_space=pltpu.VMEM), pl.BlockSpec(memory_space=pl.ANY)
    dma = pltpu.SemaphoreType.DMA
    many = dma((bands,))
    margin, weighted = pl.pallas_call(
        functools.partial(margin_kernel, bands, groups),
        name="margin",
        out_shape=(
            jax.ShapeDtypeStruct((flat, TILE), BF16),
            jax.ShapeDtypeStruct((n, cols), BF16),
        ),
        in_specs=[hbm, vmem],
        out_specs=(vmem, vmem),
        scratch_shapes=[pltpu.VMEM((n, cols), BF16), dma((1,)), many, many]
        + reduce_scratch(flat, bands, levels),
        compiler_params=pltpu.CompilerParams(
            collective_id=0, has_side_effects=True, vmem_limit_bytes=48 * 2**20),
    )(orbitals, kernel.reshape(1, width))
    return pl.pallas_call(
        functools.partial(apply_kernel, bands, groups),
        name="apply",
        out_shape=(
            jax.ShapeDtypeStruct((own, width), BF16),
            jax.ShapeDtypeStruct((bown, width), BF16),
        ),
        in_specs=[vmem, vmem, hbm],
        out_specs=(hbm, hbm),
        scratch_shapes=[
            pltpu.VMEM((n, n), F32),
            pltpu.VMEM((n, n), F32),
            pltpu.VMEM((TILE, 2 * TILE), F32),
            pltpu.VMEM((TILE, TILE), F32),
            pltpu.VMEM((n, n), BF16),
            pltpu.VMEM((n, cols), BF16),
            pltpu.VMEM((nblk, cols), BF16),
            pltpu.VMEM((nblk, cols), BF16),
            dma((2,)), many, many, dma((pieces,)), dma((pieces, bands)), many, many,
        ] + reduce_scratch(2 * n, bands, levels),
        compiler_params=pltpu.CompilerParams(
            collective_id=1, has_side_effects=True, vmem_limit_bytes=48 * 2**20),
    )(margin, weighted, block_vectors)


def solution(mesh):
    placed = (P(("img", "band"), "ga"), P("ga"), P(("img", "band"), "ga"))
    return jax.shard_map(
        shards,
        mesh=mesh,
        in_specs=placed,
        out_specs=(P(("img", "band"), "ga"), P(("img", "band"), "ga")),
        check_vma=False,
    )
```

profile of v0, /device:TPU:18, one launch (start us, length us, event | category | flops | bytes accessed | tf_op | source)
XLA Modules:
  0.0 129.1 jit_solution(11724149395631361736)
XLA Ops:
  0.6 0.0 copy-start
  0.6 1.3 copy-done
  1.9 0.0 copy-start.2
  1.9 0.7 copy-done.2
  2.6 0.0 copy-start.1
  2.6 51.2 %margin.1 = (bf16[2816,128]{1,0:T(8,128)(2,1)S(1)}, bf16[768,768]{1,0:T(8,128)(2,1)S(1)}) custom-call(bf16[192,3072]{1,0:T(8,128)(2,1)S(1)} %copy-done, f32[1,3072]{1,0:T(1,128)S(1)} %bitcast.1), custom_call_target="tpu_custom_call" | custom-call | tf_op jit(solution)/shard_map/margin/pallas_call | solution.py:374
  53.8 0.0 copy-done.1
  53.9 73.5 %apply.1 = (bf16[192,3072]{1,0:T(8,128)(2,1)S(1)}, bf16[64,3072]{1,0:T(8,128)(2,1)S(1)}) custom-call(bf16[2816,128]{1,0:T(8,128)(2,1)S(1)} %get-tuple-element.4.m_ref, bf16[768,768]{1,0:T(8,128)(2,1)S(1)} %get-tuple-element.5.w, bf16[64,3072]{1,0:T(8,128)(2,1)S(1)} %copy-done.1), custom_call_target="tpu_custom_call" | custom-call | tf_op jit(solution)/shard_map/apply/pallas_call | solution.py:388
  127.4 1.0 copy.7
  128.4 0.7 copy.8
Async XLA Ops:
  0.6 1.3 copy-start
  1.9 0.7 copy-start.2
  2.6 51.2 %copy-start.1 = (bf16[64,3072]{1,0:T(8,128)(2,1)S(1)}, bf16[64,3072]{1,0:T(8,128)(2,1)}, u32[]{:S(2)}) copy-start(bf16[64,3072]{1,0:T(8,128)(2,1)} %blk.1) | copy-start | bytes 1179652
where the time goes:
time: 130 us; the launch traced here: 129 us
  Pallas kernels  125 us (96%)
  local copies, waits for them, and re-layouts  3.73 us (3%)
    pallas_call x1, Pallas kernels, shards(): pl.pallas_call(functools.partial(apply_kernel, bands, groups), name='appl...  73.5 us
    pallas_call x1, Pallas kernels, shards(): pl.pallas_call(functools.partial(margin_kernel, bands, groups), name='mar...  51.2 us
    unnamed x8, local copies, waits for them, and re-layouts  3.73 us

commit v1 on v0

v1 whole, which is shorter than its diff:
```python
import functools

import jax
import jax.numpy as jnp
from jax import lax
from jax.experimental import pallas as pl
from jax.experimental.pallas import tpu as pltpu
from jax.sharding import PartitionSpec as P

MESH = pl.DeviceIdType.MESH
F32 = jnp.float32
BF16 = jnp.bfloat16
TILE = 128


def remote(src, dst, send_sem, recv_sem, where):
    return pltpu.make_async_remote_copy(
        src_ref=src, dst_ref=dst, send_sem=send_sem, recv_sem=recv_sem,
        device_id=where, device_id_type=MESH,
    )


def greet(places):
    barrier = pltpu.get_barrier_semaphore()
    for place in places:
        pl.semaphore_signal(barrier, inc=1, device_id=place, device_id_type=MESH)
    pl.semaphore_wait(barrier, len(places))


def dot(a, b, dims):
    return lax.dot_general(a, b, (dims, ((), ())), preferred_element_type=F32)


class Place:
    def __init__(self, bands, groups):
        self.bands = bands
        self.me = lax.axis_index("band")
        self.team = bands // 2
        self.half = self.me // self.team
        self.rank = lax.rem(self.me, self.team)
        ga = lax.axis_index("ga")
        self.core = lax.rem(ga, 2)
        self.row = lax.rem(ga // 2, 2)
        self.partner = {"ga": ga + 1 - 2 * self.core}
        self.across = {"ga": ga + 2 - 4 * self.row}
        self.peer = [lax.rem(self.me + d, bands) for d in range(bands)]
        self.far = sorted(range(1, bands), key=lambda d: -min(d, bands - d))
        self.near = self.far[::-1]
        self.bits = []
        stride = 4
        while stride < groups:
            self.bits.append({"ga": ga + stride * (1 - 2 * lax.rem(ga // stride, 2))})
            stride *= 2

    def band(self, d):
        return {"band": self.peer[d]}

    def mate(self, j):
        return lax.rem(self.rank + j, self.team)

    def rival(self, t):
        return (1 - self.half) * (self.team + t) + self.half * (self.team - 1 - t)

    def everyone(self):
        return [self.band(d) for d in range(1, self.bands)] + [self.partner, self.across] + self.bits


def span(index, size, offset=0, stride=None):
    return pl.ds(pl.multiple_of(offset + index * (stride or size), 16), size)


def reduce_scratch(rows, parts, bands, levels, sides):
    h1, h2 = rows // 2, rows // 4
    h3 = h2 // parts
    dma = pltpu.SemaphoreType.DMA
    shapes = [
        ((rows, TILE), F32), ((rows, TILE), BF16), ((h1, TILE), BF16),
        ((h1, TILE), F32), ((h1, TILE), BF16), ((h2, TILE), BF16),
        ((h2, TILE), F32), ((h2, TILE), BF16), ((parts, h3, TILE), BF16),
        ((levels, h3, TILE), BF16), ((levels, h3, TILE), BF16), ((sides * rows, TILE), BF16),
    ]
    return [pltpu.VMEM(*shape) for shape in shapes] + [
        dma((4,)), dma((parts,)), dma((parts,)), dma((levels,)), dma((levels,)),
        dma((bands,)), dma((bands,)), dma((bands,)), dma((bands,)),
        dma((2 * bands,)), dma((2 * bands,)),
    ]


SCRATCH = 23


class Reduce:
    def __init__(self, at, scratch, by_team):
        self.at = at
        (self.p32, self.p16, self.rx1, self.a32, self.a16, self.rx2, self.b32, self.b16, self.rx3,
         self.out_x, self.rx_x, self.allg, self.one, self.z_s, self.z_r, self.x_s, self.x_r,
         self.g_s, self.g_r, self.y_s, self.y_r, self.f_s, self.f_r) = scratch
        self.rows = self.p32.shape[0]
        self.h1, self.h2, self.h3 = self.rx1.shape[0], self.rx2.shape[0], self.rx3.shape[1]
        self.by_team = by_team
        if by_team:
            self.mine = at.rank
            self.parts = [(j, at.mate(j), {"band": at.half * at.team + at.mate(j)})
                          for j in range(1, at.team)]
        else:
            self.mine = at.me
            self.parts = [(d, at.peer[d], at.band(d)) for d in at.far]

    def put(self, row, value):
        size = value.shape[0]
        self.p32[row:row + size, :] = value
        self.p16[row:row + size, :] = value.astype(BF16)

    def pad(self, row):
        size = self.rows - row
        if size:
            self.put(row, jnp.zeros((size, TILE), F32))

    def to_partner(self):
        at = self.at
        return remote(self.p16.at[span(1 - at.core, self.h1)], self.rx1,
                      self.one.at[0], self.one.at[1], at.partner)

    def to_across(self):
        at = self.at
        return remote(self.a16.at[span(1 - at.row, self.h2)], self.rx2,
                      self.one.at[2], self.one.at[3], at.across)

    def to_parts(self):
        return [remote(self.b16.at[span(index, self.h3)], self.rx3.at[slot],
                       self.z_s.at[slot], self.z_r.at[slot], where)
                for slot, index, where in self.parts]

    def piece(self, d, row):
        at = self.at
        source = lax.rem(at.me + at.bands - d, at.bands)
        offset = at.core * self.h1 + row * self.h2
        if self.by_team:
            offset = offset + (source // at.team) * self.rows
            source = lax.rem(source, at.team)
        return span(source, self.h3, offset)

    def gather(self, d):
        own = self.allg.at[self.piece(0, self.at.row)]
        return remote(own, own, self.g_s.at[d], self.g_r.at[d], self.at.band(d))

    def side(self, d):
        there = self.allg.at[self.piece(d, self.at.row)]
        return remote(there, there, self.y_s.at[d], self.y_r.at[d], self.at.across)

    def last(self, d, other):
        row = 1 - self.at.row if other else self.at.row
        there = self.allg.at[self.piece(d, row)]
        e = d + self.at.bands * other
        return remote(there, there, self.f_s.at[e], self.f_r.at[e], self.at.partner)

    def s1(self):
        self.to_partner().start()

    def s2(self):
        self.to_partner().wait()
        self.a32[...] = self.p32[span(self.at.core, self.h1), :] + self.rx1[...].astype(F32)
        self.a16[...] = self.a32[...].astype(BF16)
        self.to_across().start()

    def s3(self):
        self.to_across().wait()
        self.b32[...] = self.a32[span(self.at.row, self.h2), :] + self.rx2[...].astype(F32)
        self.b16[...] = self.b32[...].astype(BF16)
        for copy in self.to_parts():
            copy.start()

    def s4(self):
        at = self.at
        for copy in self.to_parts():
            copy.wait()
        total = self.b32[span(self.mine, self.h3), :]
        for slot, _, _ in self.parts:
            total = total + self.rx3[slot].astype(F32)
        for i, place in enumerate(at.bits):
            self.out_x[i] = total.astype(BF16)
            copy = remote(self.out_x.at[i], self.rx_x.at[i], self.x_s.at[i], self.x_r.at[i], place)
            copy.start()
            copy.wait()
            total = self.out_x[i].astype(F32) + self.rx_x[i].astype(F32)
        self.allg[self.piece(0, at.row), :] = total.astype(BF16)
        for d in at.far:
            self.gather(d).start()
        self.side(0).start()
        self.last(0, 0).start()

    def s5(self):
        for d in self.at.near:
            self.gather(d).wait()
            self.side(d).start()
            self.last(d, 0).start()

    def s6(self):
        for d in [0] + self.at.near:
            self.side(d).wait()
            self.last(d, 1).start()

    def s7(self):
        for d in [0] + self.at.near:
            self.last(d, 0).wait()
            self.last(d, 1).wait()


def split(a):
    high = a.astype(BF16)
    return high, (a - high.astype(F32)).astype(BF16)


def product3(a, b, dims):
    (ah, al), (bh, bl) = split(a), split(b)
    return dot(ah, bh, dims) + (dot(ah, bl, dims) + dot(al, bh, dims))


def identity(rows):
    shape = (rows, rows)
    return (lax.broadcasted_iota(jnp.int32, shape, 0)
            == lax.broadcasted_iota(jnp.int32, shape, 1)).astype(F32)


def factor_tile(d_ref, t_ref, hooks):
    G, SUB, BLK = 32, 8, 16
    H, K = G // SUB, BLK // SUB
    sub = lax.broadcasted_iota(jnp.int32, (SUB, TILE), 0)

    def spread(block, i):
        return jnp.broadcast_to(block[i:i + 1, :], (SUB, TILE))

    def lane(block, c):
        where = jnp.broadcast_to(c, (SUB, TILE))
        return jnp.take_along_axis(block, where, axis=1, mode="promise_in_bounds")

    def step(g, carry):
        start = pl.multiple_of(g * G, G)
        lefts = [d_ref[pl.ds(start + h * SUB, SUB), 0:TILE] for h in range(H)]
        rights = [d_ref[pl.ds(start + h * SUB, SUB), TILE:2 * TILE] for h in range(H)]
        us, vs = [], []
        for b in range(G // BLK):
            h0 = b * K
            cols = [{h: lane(lefts[h], start + (b * BLK + c)) for h in range(h0 + c // SUB, H)}
                    for c in range(BLK)]
            low = [[None] * BLK for _ in range(BLK)]
            u, v = [], []
            u_rows = [jnp.zeros((SUB, TILE), F32) for _ in range(K)]
            v_rows = [jnp.zeros((SUB, TILE), F32) for _ in range(K)]
            for j in range(BLK):
                k, i = j // SUB, j % SUB
                r = lax.rsqrt(spread(cols[j][h0 + k], i))
                for h in range(h0 + k, H):
                    cols[j][h] = cols[j][h] * r
                for c in range(j + 1, BLK):
                    low[c][j] = spread(cols[j][h0 + c // SUB], c % SUB)
                    for h in range(h0 + c // SUB, H):
                        cols[c][h] = cols[c][h] - cols[j][h] * low[c][j]
                p, q = spread(lefts[h0 + k], i), spread(rights[h0 + k], i)
                for t in range(j):
                    p = p - low[j][t] * u[t]
                    q = q - low[j][t] * v[t]
                u.append(p * r)
                v.append(q * r)
                u_rows[k] = jnp.where(sub == i, u[j], u_rows[k])
                v_rows[k] = jnp.where(sub == i, v[j], v_rows[k])
            us += u_rows
            vs += v_rows
            for h in range(h0 + K, H):
                for j in range(BLK):
                    lefts[h] = lefts[h] - cols[j][h] * u[j]
                    rights[h] = rights[h] - cols[j][h] * v[j]
        u_all = jnp.concatenate(us, axis=0)
        v_all = jnp.concatenate(vs, axis=0)
        t_ref[pl.ds(start, G), :] = v_all
        both = jnp.concatenate([u_all, v_all], axis=1)
        high = both.astype(BF16).astype(F32)
        low = both - high
        lhs = jnp.concatenate([high[:, :TILE], high[:, :TILE], low[:, :TILE]], axis=0)
        rhs = jnp.concatenate([high, low, high], axis=0)
        d_ref[...] -= dot(lhs.astype(BF16), rhs.astype(BF16), ((0,), (0,)))
        for k, hook in enumerate(hooks):
            if hook is not None:
                pl.when(g == k)(hook)
        return carry

    lax.fori_loop(0, TILE // G, step, 0)


def ace_kernel(bands, groups, orb, kern, blk, ace, exch, full, extra, w, wx, a, rest, x16, xlow, mba,
               d_ref, t_ref, proj, bfull, acc, applied, loc, m_s, m_r, n_s, n_r, c_s, c_r,
               b_s, b_r, p_s, p_r, e_s, e_r, *scratch):
    at = Place(bands, groups)
    me, team = at.me, at.team
    own, bown = ace.shape[0], exch.shape[0]
    cols = w.shape[1]
    n, nblk = own * bands, bown * bands
    n2 = n // 2
    scale = 1.0 / (ace.shape[1] * groups)
    inner = Reduce(at, scratch[:SCRATCH], True)
    cross = Reduce(at, scratch[SCRATCH:2 * SCRATCH], False)
    couple = Reduce(at, scratch[2 * SCRATCH:], False)
    greet(at.everyone())

    def chunk(index):
        return pl.ds(pl.multiple_of(index * cols, TILE), cols)

    def twin(index):
        return chunk(lax.rem(index + team, bands))

    mine = full.at[span(me, own)]
    also = extra.at[span(at.rank, own)]
    bmine = bfull.at[span(me, bown)]

    def kept():
        return [pltpu.make_async_copy(orb.at[:, chunk(me)], mine, loc.at[0]),
                pltpu.make_async_copy(orb.at[:, twin(me)], also, loc.at[1])]

    def to_mates():
        copies = []
        for j in range(1, team):
            p = at.half * team + at.mate(j)
            copies.append(remote(orb.at[:, chunk(p)], mine, m_s.at[j], m_r.at[j], {"band": p}))
            copies.append(remote(orb.at[:, twin(p)], also, n_s.at[j], n_r.at[j], {"band": p}))
        return copies

    def to_rival(t, sender):
        p = at.rival(t)
        return remote(orb.at[:, chunk(p)], mine, c_s.at[t], c_r.at[sender], {"band": p})

    def blocks():
        return [remote(blk.at[:, chunk(at.peer[d])], bmine, b_s.at[d], b_r.at[d], at.band(d))
                for d in at.far]

    def bkept():
        return pltpu.make_async_copy(blk.at[:, chunk(me)], bmine, loc.at[2])

    for copy in to_mates():
        copy.start()
    for t in range(team):
        to_rival(t, at.rank).start()
    for copy in kept():
        copy.start()
    bkept().start()

    def weigh(rows, columns):
        return (-(rows.astype(F32) * kern[:, columns])).astype(BF16)

    for copy in kept() + to_mates():
        copy.wait()
    band = span(at.half, n2)
    w[band, :] = weigh(full[band, :], chunk(me))
    wx[...] = weigh(extra[...], twin(me))
    row = 0
    for s in range(0, n2, TILE):
        e = s + TILE
        product = (dot(w[span(at.half, TILE, s, n2), :], full[span(at.half, e, 0, n2), :],
                       ((1,), (1,)))
                   + dot(wx[s:e, :], extra[0:e, :], ((1,), (1,))))
        for c in range(0, e, TILE):
            inner.put(row, product[:, c:c + TILE])
            row += TILE
    inner.pad(row)
    inner.s1()
    inner.s2()
    inner.s3()
    inner.s4()
    for copy in blocks():
        copy.start()
    for t in range(team):
        to_rival(t, t).wait_recv()
    other = span(1 - at.half, n2)
    w[other, :] = weigh(full[other, :], chunk(me))
    row = 0
    for s in range(n2, n, TILE):
        product = dot(w[s:s + TILE, :], full[0:n2, :], ((1,), (1,)))
        for c in range(0, n2, TILE):
            cross.put(row, product[:, c:c + TILE])
            row += TILE
    cross.pad(row)
    cross.s1()
    inner.s5()
    cross.s2()
    inner.s6()
    inner.s7()
    row = 0
    for base in (0, n2):
        for s in range(base, base + n2, TILE):
            for c in range(base, s + TILE, TILE):
                a[s:s + TILE, c:c + TILE] = inner.allg[row:row + TILE, :].astype(F32) * -scale
                row += TILE
        row = inner.rows
    rest[...] = identity(n)
    x16[...] = jnp.zeros_like(x16)

    def couple_start():
        bkept().wait()
        for copy in blocks():
            copy.wait()
        half = nblk // 2
        for h in range(2):
            couple.put(h * n, dot(w[...], bfull[h * half:(h + 1) * half, :], ((1,), (1,))))
        couple.s1()

    cuts = sorted(set(range(0, n, TILE)) | set(range(0, n, own)) | {n})
    pieces = list(enumerate(zip(cuts[:-1], cuts[1:])))

    def piece(q, r0, r1, source, target):
        lo = r0 % own
        return remote(proj.at[r0:r1], ace.at[lo:lo + r1 - r0, chunk(source)],
                      p_s.at[q], p_r.at[q, source], {"band": target})

    def stay(q, r0, r1):
        lo = r0 % own
        return pltpu.make_async_copy(
            proj.at[r0:r1], ace.at[lo:lo + r1 - r0, chunk(me)], p_s.at[q])

    def deliver(lo, hi):
        for q, (r0, r1) in pieces:
            if lo <= r0 < hi:
                owner = r0 // own

                @pl.when(me != owner)
                def _():
                    piece(q, r0, r1, me, owner).start()

                @pl.when(me == owner)
                def _():
                    stay(q, r0, r1).start()

    tiles = n2 // TILE
    first = [cross.s3, couple_start, cross.s4, couple.s2, cross.s5, couple.s3, cross.s6]
    slots = [(0, 1), (1, 0), (1, 1), (1, 2), (2, 0), (2, 1), (2, 2)]
    hooks = [[None] * 4 for _ in range(2 * tiles)]
    for (k, g), stage in zip(slots, first):
        hooks[min(k, tiles - 1)][g] = stage
    hooks[tiles][0], hooks[tiles][1], hooks[tiles][3] = couple.s5, couple.s6, couple.s7

    def attach(lo, hi):
        half = nblk // 2
        for h in range(2):
            part = allg_dot(lo, hi, h) * scale
            update = dot(part.astype(BF16), proj[lo:hi, :], ((0,), (0,)))
            if lo == 0:
                acc[h * half:(h + 1) * half, :] = update
            else:
                acc[h * half:(h + 1) * half, :] += update

    def allg_dot(lo, hi, h):
        return dot(x16[lo:hi, 0:hi], couple.allg[h * n:h * n + hi, :], ((1,), (0,)))

    for k, s in enumerate(range(0, n, TILE)):
        e = s + TILE
        top = n2 if s < n2 else n
        d_ref[:, 0:TILE] = a[s:e, s:e]
        d_ref[:, TILE:] = identity(TILE)
        factor_tile(d_ref, t_ref, hooks[k])
        tile = t_ref[...]
        rows = product3(tile, rest[s:e, 0:e], ((1,), (0,)))
        high, low = split(rows)
        x16[s:e, 0:e] = high
        if s < n2:
            xlow[s:e, 0:n2] = jnp.zeros((TILE, n2), BF16)
            xlow[s:e, 0:e] = low
        proj[s:e, :] = (dot(high, w[0:e, :], ((1,), (0,)))
                        + dot(low, w[0:e, :], ((1,), (0,)))).astype(BF16)
        if s >= n2:
            deliver(s, e)
        if e < top:
            panel = product3(a[e:top, s:e], tile, ((1,), (1,)))
            for c in range(e, top, TILE):
                a[c:top, c:c + TILE] -= product3(panel[c - e:], panel[c - e:c - s], ((1,), (1,)))
            rest[e:top, 0:e] -= product3(panel, rows, ((1,), (0,)))
        if e == n2:
            cross.s7()
            row = 0
            for r in range(0, n2, TILE):
                for c in range(0, n2, TILE):
                    mba[r:r + TILE, c:c + TILE] = cross.allg[row:row + TILE, :]
                    row += TILE
            both = (((1,), (1,)))
            below = (dot(mba[...], x16[0:n2, 0:n2], both) + dot(mba[...], xlow[...], both)) * -scale
            bh, bl = split(below)
            for c in range(0, n2, TILE):
                d = c + TILE
                a[n2 + c:n, n2 + c:n2 + d] -= (
                    dot(bh[c:], bh[c:d], both) + (dot(bh[c:], bl[c:d], both) + dot(bl[c:], bh[c:d], both)))
            over = ((1,), (0,))
            xh = x16[0:n2, 0:n2]
            rest[n2:, 0:n2] = -(dot(bh, xh, over) + (dot(bh, xlow[...], over) + dot(bl, xh, over)))
            couple.s4()
            deliver(0, n2)
        if e == n - TILE:
            attach(0, e)
    attach(n - TILE, n)
    applied[...] = (-acc[...]).astype(BF16)
    outs = [remote(applied.at[span(at.peer[d], bown)], exch.at[:, chunk(me)],
                   e_s.at[d], e_r.at[d], at.band(d)) for d in at.far]
    outs.append(pltpu.make_async_copy(applied.at[span(me, bown)], exch.at[:, chunk(me)], loc.at[3]))
    for copy in outs:
        copy.start()
    for t in range(team):
        to_rival(t, t).wait_send()
    for q, (r0, r1) in pieces:
        owner = r0 // own

        @pl.when(me != owner)
        def _():
            piece(q, r0, r1, me, owner).wait_send()

        @pl.when(me == owner)
        def _():
            stay(q, r0, r1).wait()
            for d in range(1, bands):
                piece(q, r0, r1, at.peer[d], at.peer[d]).wait_recv()
    for copy in outs:
        copy.wait()


def shards(orbitals, kernel, block_vectors):
    groups, bands = lax.axis_size("ga"), lax.axis_size("band")
    own, width = orbitals.shape
    bown = block_vectors.shape[0]
    cols = width // bands
    n, nblk = own * bands, bown * bands
    n2, team = n // 2, bands // 2
    levels = max(groups.bit_length() - 3, 1)
    tiles = n2 // TILE

    def padded(rows, parts):
        unit = 4 * parts * 16
        return -(-rows // unit) * unit

    pieces = len(set(range(0, n, TILE)) | set(range(0, n, own)))
    vmem, hbm = pl.BlockSpec(memory_space=pltpu.VMEM), pl.BlockSpec(memory_space=pl.ANY)
    dma = pltpu.SemaphoreType.DMA
    many, some = dma((bands,)), dma((team,))
    return pl.pallas_call(
        functools.partial(ace_kernel, bands, groups),
        name="ace",
        out_shape=(
            jax.ShapeDtypeStruct((own, width), BF16),
            jax.ShapeDtypeStruct((bown, width), BF16),
        ),
        in_specs=[hbm, vmem, hbm],
        out_specs=(hbm, hbm),
        scratch_shapes=[
            pltpu.VMEM((n, cols), BF16),
            pltpu.VMEM((n2, cols), BF16),
            pltpu.VMEM((n, cols), BF16),
            pltpu.VMEM((n2, cols), BF16),
            pltpu.VMEM((n, n), F32),
            pltpu.VMEM((n, n), F32),
            pltpu.VMEM((n, n), BF16),
            pltpu.VMEM((n2, n2), BF16),
            pltpu.VMEM((n2, n2), BF16),
            pltpu.VMEM((TILE, 2 * TILE), F32),
            pltpu.VMEM((TILE, TILE), F32),
            pltpu.VMEM((n, cols), BF16),
            pltpu.VMEM((nblk, cols), BF16),
            pltpu.VMEM((nblk, cols), F32),
            pltpu.VMEM((nblk, cols), BF16),
            dma((4,)), some, some, some, some, some, some,
            many, many, dma((pieces,)), dma((pieces, bands)), many, many,
        ]
        + reduce_scratch(padded(tiles * (tiles + 1) // 2 * TILE, team), team, bands, levels, 2)
        + reduce_scratch(padded(tiles * tiles * TILE, bands), bands, bands, levels, 1)
        + reduce_scratch(2 * n, bands, bands, levels, 1),
        compiler_params=pltpu.CompilerParams(
            collective_id=0, has_side_effects=True, vmem_limit_bytes=56 * 2**20),
    )(orbitals, kernel.reshape(1, width), block_vectors)


def solution(mesh):
    placed = (P(("img", "band"), "ga"), P("ga"), P(("img", "band"), "ga"))
    return jax.shard_map(
        shards,
        mesh=mesh,
        in_specs=placed,
        out_specs=(P(("img", "band"), "ga"), P(("img", "band"), "ga")),
        check_vma=False,
    )
```

time: 130 us -> 123 us (0.946)
  Pallas kernels: 125 us -> 119 us
    pallas_call x2 -> x1, Pallas kernels: 125 us -> 119 us  [shards(): pl.pallas_call(functools.partial(ace_kernel, bands, groups), name='ace',...]
    unnamed x8 -> x4, local copies, waits for them, and re-layouts: 3.73 us -> 3.16 us
where the time goes in v1:
time: 123 us; the launch traced here: 122 us
  Pallas kernels  119 us (97%)
  local copies, waits for them, and re-layouts  3.16 us (3%)
    pallas_call x1, Pallas kernels, shards(): pl.pallas_call(functools.partial(ace_kernel, bands, groups), name='ace',...  119 us
    unnamed x4, local copies, waits for them, and re-layouts  3.16 us

profile of v1, /device:TPU:18, one launch (start us, length us, event | category | flops | bytes accessed | tf_op | source)
XLA Modules:
  0.0 122.4 jit_solution(5390362489882577380)
XLA Ops:
  0.6 118.5 %ace.1 = (bf16[192,3072]{1,0:T(8,128)(2,1)}, bf16[64,3072]{1,0:T(8,128)(2,1)}) custom-call(bf16[192,3072]{1,0:T(8,128)(2,1)} %orb.1, f32[1,3072]{1,0:T(1,128)} %bitcast.1, bf16[64,3072]{1,0:T(8,128)(2,1)} %blk.1), custom_call_target="tpu_custom_call" | custom-call | tf_op jit(solution)/shard_map/ace/pallas_call | solution.py:538
  119.2 0.0 copy-start
  119.2 2.4 %copy.7 = bf16[192,3072]{1,0:T(8,128)(2,1)} copy(bf16[192,3072]{1,0:T(8,128)(2,1)} %get-tuple-element.4) | data formatting | bytes 2359296
  121.6 0.0 copy-done
  121.6 0.7 copy.8
Async XLA Ops:
  119.2 2.4 %copy-start = (bf16[64,3072]{1,0:T(8,128)(2,1)S(1)}, bf16[64,3072]{1,0:T(8,128)(2,1)}, u32[]{:S(2)}) copy-start(bf16[64,3072]{1,0:T(8,128)(2,1)} %get-tuple-element.5) | copy-start | bytes 1179652

commit v2 on v1

--- a/solution.py
+++ b/solution.py
@@ -11,6 +11,7 @@
 F32 = jnp.float32
 BF16 = jnp.bfloat16
 TILE = 128
+SLICE = 16
 
 
 def remote(src, dst, send_sem, recv_sem, where):
@@ -279,17 +280,20 @@
         lhs = jnp.concatenate([high[:, :TILE], high[:, :TILE], low[:, :TILE]], axis=0)
         rhs = jnp.concatenate([high, low, high], axis=0)
         d_ref[...] -= dot(lhs.astype(BF16), rhs.astype(BF16), ((0,), (0,)))
-        for k, hook in enumerate(hooks):
-            if hook is not None:
-                pl.when(g == k)(hook)
+        for k, stages in enumerate(hooks):
+            if stages:
+                @pl.when(g == k)
+                def _():
+                    for stage in stages:
+                        stage()
         return carry
 
     lax.fori_loop(0, TILE // G, step, 0)
 
 
 def ace_kernel(bands, groups, orb, kern, blk, ace, exch, full, extra, w, wx, a, rest, x16, xlow, mba,
-               d_ref, t_ref, proj, bfull, acc, applied, loc, m_s, m_r, n_s, n_r, c_s, c_r,
-               b_s, b_r, p_s, p_r, e_s, e_r, *scratch):
+               d_ref, t_ref, proj, proj2, bfull, acc, applied, loc, m_s, m_r, n_s, n_r, c_s, c_r,
+               d_s, d_r, b_s, b_r, p_s, p_r, t_s, t_r, e_s, e_r, *scratch):
     at = Place(bands, groups)
     me, team = at.me, at.team
     own, bown = ace.shape[0], exch.shape[0]
@@ -309,7 +313,7 @@
         return chunk(lax.rem(index + team, bands))
 
     mine = full.at[span(me, own)]
-    also = extra.at[span(at.rank, own)]
+    also = extra.at[span(me, own)]
     bmine = bfull.at[span(me, bown)]
 
     def kept():
@@ -328,6 +332,22 @@
         p = at.rival(t)
         return remote(orb.at[:, chunk(p)], mine, c_s.at[t], c_r.at[sender], {"band": p})
 
+    def twin_rival(t, sender, lo=0, size=own):
+        p = at.rival(t)
+        return remote(orb.at[pl.ds(lo, size), twin(p)], extra.at[span(me, size, lo, own)],
+                      d_s.at[t], d_r.at[sender], {"band": p})
+
+    slices = [(t, lo) for lo in range(0, own, SLICE) for t in range(team)]
+
+    def upward(count):
+        def go():
+            @pl.when(at.half == 0)
+            def _():
+                for t, lo in batch:
+                    twin_rival(t, at.rank, lo, SLICE).start()
+        batch, slices[:] = slices[:count], slices[count:]
+        return go
+
     def blocks():
         return [remote(blk.at[:, chunk(at.peer[d])], bmine, b_s.at[d], b_r.at[d], at.band(d))
                 for d in at.far]
@@ -350,13 +370,14 @@
         copy.wait()
     band = span(at.half, n2)
     w[band, :] = weigh(full[band, :], chunk(me))
-    wx[...] = weigh(extra[...], twin(me))
+    wx[band, :] = weigh(extra[band, :], twin(me))
     row = 0
     for s in range(0, n2, TILE):
         e = s + TILE
         product = (dot(w[span(at.half, TILE, s, n2), :], full[span(at.half, e, 0, n2), :],
                        ((1,), (1,)))
-                   + dot(wx[s:e, :], extra[0:e, :], ((1,), (1,))))
+                   + dot(wx[span(at.half, TILE, s, n2), :], extra[span(at.half, e, 0, n2), :],
+                         ((1,), (1,))))
         for c in range(0, e, TILE):
             inner.put(row, product[:, c:c + TILE])
             row += TILE
@@ -365,8 +386,6 @@
     inner.s2()
     inner.s3()
     inner.s4()
-    for copy in blocks():
-        copy.start()
     for t in range(team):
         to_rival(t, t).wait_recv()
     other = span(1 - at.half, n2)
@@ -380,6 +399,8 @@
     cross.pad(row)
     cross.s1()
     inner.s5()
+    for copy in blocks():
+        copy.start()
     cross.s2()
     inner.s6()
     inner.s7()
@@ -392,6 +413,7 @@
         row = inner.rows
     rest[...] = identity(n)
     x16[...] = jnp.zeros_like(x16)
+    xlow[...] = jnp.zeros_like(xlow)
 
     def couple_start():
         bkept().wait()
@@ -405,36 +427,71 @@
     cuts = sorted(set(range(0, n, TILE)) | set(range(0, n, own)) | {n})
     pieces = list(enumerate(zip(cuts[:-1], cuts[1:])))
 
-    def piece(q, r0, r1, source, target):
+    def piece(q, r0, r1, source, target, other):
         lo = r0 % own
-        return remote(proj.at[r0:r1], ace.at[lo:lo + r1 - r0, chunk(source)],
-                      p_s.at[q], p_r.at[q, source], {"band": target})
-
-    def stay(q, r0, r1):
+        rows, sent, got = (proj2, t_s, t_r) if other else (proj, p_s, p_r)
+        where = twin(source) if other else chunk(source)
+        return remote(rows.at[r0:r1], ace.at[lo:lo + r1 - r0, where],
+                      sent.at[q], got.at[q, source], {"band": target})
+
+    def stay(q, r0, r1, other):
         lo = r0 % own
-        return pltpu.make_async_copy(
-            proj.at[r0:r1], ace.at[lo:lo + r1 - r0, chunk(me)], p_s.at[q])
-
-    def deliver(lo, hi):
+        rows, sent = (proj2, t_s) if other else (proj, p_s)
+        where = twin(me) if other else chunk(me)
+        return pltpu.make_async_copy(rows.at[r0:r1], ace.at[lo:lo + r1 - r0, where], sent.at[q])
+
+    def deliver(lo, hi, other):
         for q, (r0, r1) in pieces:
             if lo <= r0 < hi:
                 owner = r0 // own
 
-                @pl.when(me != owner)
+                @pl.when((me != owner) & (at.half == owner // team))
                 def _():
-                    piece(q, r0, r1, me, owner).start()
+                    piece(q, r0, r1, me, owner, other).start()
 
                 @pl.when(me == owner)
                 def _():
-                    stay(q, r0, r1).start()
+                    stay(q, r0, r1, other).start()
+
+    def project(lo, hi):
+        proj2[lo:hi, :] = (dot(x16[lo:hi, 0:hi], wx[0:hi, :], ((1,), (0,)))
+                           + dot(xlow[lo:hi, 0:hi], wx[0:hi, :], ((1,), (0,)))).astype(BF16)
+
+    def spare():
+        @pl.when(at.half == 0)
+        def _():
+            project(0, n2)
+
+        for other in (0, 1):
+            deliver(0, n2, other)
+
+    def arrive():
+        @pl.when(at.half == 1)
+        def _():
+            for t in range(team):
+                twin_rival(t, t).wait_recv()
+            wx[0:n2, :] = weigh(extra[0:n2, :], twin(me))
 
     tiles = n2 // TILE
-    first = [cross.s3, couple_start, cross.s4, couple.s2, cross.s5, couple.s3, cross.s6]
-    slots = [(0, 1), (1, 0), (1, 1), (1, 2), (2, 0), (2, 1), (2, 2)]
-    hooks = [[None] * 4 for _ in range(2 * tiles)]
-    for (k, g), stage in zip(slots, first):
-        hooks[min(k, tiles - 1)][g] = stage
-    hooks[tiles][0], hooks[tiles][1], hooks[tiles][3] = couple.s5, couple.s6, couple.s7
+    hooks = [[[] for _ in range(4)] for _ in range(2 * tiles)]
+
+    def at_hook(k, g, *stages):
+        hooks[k][g] += stages
+
+    for g in range(4):
+        at_hook(0, g, upward(1))
+        at_hook(tiles - 2, g, upward(1))
+        at_hook(tiles - 1, g, upward(1))
+    at_hook(0, 1, cross.s3)
+    at_hook(tiles - 2, 0, couple_start)
+    at_hook(tiles - 2, 1, cross.s4)
+    at_hook(tiles - 2, 3, couple.s2)
+    at_hook(tiles - 1, 0, cross.s5)
+    at_hook(tiles - 1, 1, couple.s3)
+    at_hook(tiles - 1, 2, cross.s6)
+    at_hook(tiles, 1, couple.s5, upward(len(slices)), spare)
+    at_hook(tiles, 3, couple.s6)
+    at_hook(tiles + 1, 0, couple.s7)
 
     def attach(lo, hi):
         half = nblk // 2
@@ -459,13 +516,11 @@
         rows = product3(tile, rest[s:e, 0:e], ((1,), (0,)))
         high, low = split(rows)
         x16[s:e, 0:e] = high
-        if s < n2:
-            xlow[s:e, 0:n2] = jnp.zeros((TILE, n2), BF16)
-            xlow[s:e, 0:e] = low
+        xlow[s:e, 0:e] = low
         proj[s:e, :] = (dot(high, w[0:e, :], ((1,), (0,)))
                         + dot(low, w[0:e, :], ((1,), (0,)))).astype(BF16)
         if s >= n2:
-            deliver(s, e)
+            deliver(s, e, 0)
         if e < top:
             panel = product3(a[e:top, s:e], tile, ((1,), (1,)))
             for c in range(e, top, TILE):
@@ -479,7 +534,7 @@
                     mba[r:r + TILE, c:c + TILE] = cross.allg[row:row + TILE, :]
                     row += TILE
             both = (((1,), (1,)))
-            below = (dot(mba[...], x16[0:n2, 0:n2], both) + dot(mba[...], xlow[...], both)) * -scale
+            below = (dot(mba[...], x16[0:n2, 0:n2], both) + dot(mba[...], xlow[0:n2, 0:n2], both)) * -scale
             bh, bl = split(below)
             for c in range(0, n2, TILE):
                 d = c + TILE
@@ -487,9 +542,8 @@
                     dot(bh[c:], bh[c:d], both) + (dot(bh[c:], bl[c:d], both) + dot(bl[c:], bh[c:d], both)))
             over = ((1,), (0,))
             xh = x16[0:n2, 0:n2]
-            rest[n2:, 0:n2] = -(dot(bh, xh, over) + (dot(bh, xlow[...], over) + dot(bl, xh, over)))
+            rest[n2:, 0:n2] = -(dot(bh, xh, over) + (dot(bh, xlow[0:n2, 0:n2], over) + dot(bl, xh, over)))
             couple.s4()
-            deliver(0, n2)
         if e == n - TILE:
             attach(0, e)
     attach(n - TILE, n)
@@ -499,20 +553,36 @@
     outs.append(pltpu.make_async_copy(applied.at[span(me, bown)], exch.at[:, chunk(me)], loc.at[3]))
     for copy in outs:
         copy.start()
+    arrive()
+
+    @pl.when(at.half == 1)
+    def _():
+        project(n2, n)
+
+    deliver(n2, n, 1)
     for t in range(team):
         to_rival(t, t).wait_send()
+
+    @pl.when(at.half == 0)
+    def _():
+        for t in range(team):
+            twin_rival(t, t).wait_send()
+
     for q, (r0, r1) in pieces:
         owner = r0 // own
 
-        @pl.when(me != owner)
+        @pl.when((me != owner) & (at.half == owner // team))
         def _():
-            piece(q, r0, r1, me, owner).wait_send()
+            for other in (0, 1):
+                piece(q, r0, r1, me, owner, other).wait_send()
 
         @pl.when(me == owner)
         def _():
-            stay(q, r0, r1).wait()
-            for d in range(1, bands):
-                piece(q, r0, r1, at.peer[d], at.peer[d]).wait_recv()
+            for other in (0, 1):
+                stay(q, r0, r1, other).wait()
+                for j in range(1, team):
+                    mate = at.half * team + at.mate(j)
+                    piece(q, r0, r1, mate, mate, other).wait_recv()
     for copy in outs:
         copy.wait()
 
@@ -546,22 +616,24 @@
         out_specs=(hbm, hbm),
         scratch_shapes=[
             pltpu.VMEM((n, cols), BF16),
-            pltpu.VMEM((n2, cols), BF16),
             pltpu.VMEM((n, cols), BF16),
-            pltpu.VMEM((n2, cols), BF16),
+            pltpu.VMEM((n, cols), BF16),
+            pltpu.VMEM((n, cols), BF16),
             pltpu.VMEM((n, n), F32),
             pltpu.VMEM((n, n), F32),
             pltpu.VMEM((n, n), BF16),
-            pltpu.VMEM((n2, n2), BF16),
+            pltpu.VMEM((n, n), BF16),
             pltpu.VMEM((n2, n2), BF16),
             pltpu.VMEM((TILE, 2 * TILE), F32),
             pltpu.VMEM((TILE, TILE), F32),
             pltpu.VMEM((n, cols), BF16),
+            pltpu.VMEM((n, cols), BF16),
             pltpu.VMEM((nblk, cols), BF16),
             pltpu.VMEM((nblk, cols), F32),
             pltpu.VMEM((nblk, cols), BF16),
-            dma((4,)), some, some, some, some, some, some,
-            many, many, dma((pieces,)), dma((pieces, bands)), many, many,
+            dma((4,)), some, some, some, some, some, some, some, some,
+            many, many, dma((pieces,)), dma((pieces, bands)), dma((pieces,)), dma((pieces, bands)),
+            many, many,
         ]
         + reduce_scratch(padded(tiles * (tiles + 1) // 2 * TILE, team), team, bands, levels, 2)
         + reduce_scratch(padded(tiles * tiles * TILE, bands), bands, bands, levels, 1)

time: 123 us -> 105 us (0.85)
  Pallas kernels: 119 us -> 100 us
    pallas_call x1, Pallas kernels: 119 us -> 100 us  [shards(): pl.pallas_call(functools.partial(ace_kernel, bands, groups), name='ace',...]
where the time goes in v2:
time: 105 us; the launch traced here: 104 us
  Pallas kernels  100 us (95%)
  local copies, waits for them, and re-layouts  3.16 us (3%)
    pallas_call x1, Pallas kernels, shards(): pl.pallas_call(functools.partial(ace_kernel, bands, groups), name='ace',...  100 us
    unnamed x4, local copies, waits for them, and re-layouts  3.16 us

profile of v2, /device:TPU:18, one launch (start us, length us, event | category | flops | bytes accessed | tf_op | source)
XLA Modules:
  0.0 104.0 jit_solution(8640442119920342012)
XLA Ops:
  0.6 100.2 %ace.1 = (bf16[192,3072]{1,0:T(8,128)(2,1)}, bf16[64,3072]{1,0:T(8,128)(2,1)}) custom-call(bf16[192,3072]{1,0:T(8,128)(2,1)} %orb.1, f32[1,3072]{1,0:T(1,128)} %bitcast.1, bf16[64,3072]{1,0:T(8,128)(2,1)} %blk.1), custom_call_target="tpu_custom_call" | custom-call | tf_op jit(solution)/shard_map/ace/pallas_call | solution.py:608
  100.8 0.0 copy-start
  100.8 2.4 %copy.7 = bf16[192,3072]{1,0:T(8,128)(2,1)} copy(bf16[192,3072]{1,0:T(8,128)(2,1)} %get-tuple-element.4) | data formatting | bytes 2359296
  103.3 0.0 copy-done
  103.3 0.7 copy.8
Async XLA Ops:
  100.8 2.4 %copy-start = (bf16[64,3072]{1,0:T(8,128)(2,1)S(1)}, bf16[64,3072]{1,0:T(8,128)(2,1)}, u32[]{:S(2)}) copy-start(bf16[64,3072]{1,0:T(8,128)(2,1)} %get-tuple-element.5) | copy-start | bytes 1179652

commit v3 on v2

--- a/solution.py
+++ b/solution.py
@@ -11,7 +11,7 @@
 F32 = jnp.float32
 BF16 = jnp.bfloat16
 TILE = 128
-SLICE = 16
+LANES = 128
 
 
 def remote(src, dst, send_sem, recv_sem, where):
@@ -232,55 +232,52 @@
         return jnp.broadcast_to(block[i:i + 1, :], (SUB, TILE))
 
     def lane(block, c):
-        where = jnp.broadcast_to(c, (SUB, TILE))
+        where = jnp.full((SUB, TILE), c, jnp.int32)
         return jnp.take_along_axis(block, where, axis=1, mode="promise_in_bounds")
 
     def step(g, carry):
-        start = pl.multiple_of(g * G, G)
+        start = g * G if isinstance(g, int) else pl.multiple_of(g * G, G)
         lefts = [d_ref[pl.ds(start + h * SUB, SUB), 0:TILE] for h in range(H)]
         rights = [d_ref[pl.ds(start + h * SUB, SUB), TILE:2 * TILE] for h in range(H)]
-        us, vs = [], []
+        us, vs = [None] * H, [None] * H
         for b in range(G // BLK):
             h0 = b * K
             cols = [{h: lane(lefts[h], start + (b * BLK + c)) for h in range(h0 + c // SUB, H)}
                     for c in range(BLK)]
-            low = [[None] * BLK for _ in range(BLK)]
-            u, v = [], []
-            u_rows = [jnp.zeros((SUB, TILE), F32) for _ in range(K)]
-            v_rows = [jnp.zeros((SUB, TILE), F32) for _ in range(K)]
+            pivot = spread(cols[0][h0], 0)
             for j in range(BLK):
-                k, i = j // SUB, j % SUB
-                r = lax.rsqrt(spread(cols[j][h0 + k], i))
-                for h in range(h0 + k, H):
+                k, i = h0 + j // SUB, j % SUB
+                r = lax.rsqrt(pivot)
+                low = {c: spread(cols[j][h0 + c // SUB], c % SUB) for c in range(j + 1, BLK)}
+                if j + 1 < BLK:
+                    low[j + 1] = low[j + 1] * r
+                    pivot = spread(cols[j + 1][h0 + (j + 1) // SUB], (j + 1) % SUB) - low[j + 1] * low[j + 1]
+                for h in range(k, H):
                     cols[j][h] = cols[j][h] * r
+                u, v = spread(lefts[k], i) * r, spread(rights[k], i) * r
+                us[k] = u if i == 0 else jnp.where(sub == i, u, us[k])
+                vs[k] = v if i == 0 else jnp.where(sub == i, v, vs[k])
                 for c in range(j + 1, BLK):
-                    low[c][j] = spread(cols[j][h0 + c // SUB], c % SUB)
+                    scaled = low[c] if c == j + 1 else low[c] * r
                     for h in range(h0 + c // SUB, H):
-                        cols[c][h] = cols[c][h] - cols[j][h] * low[c][j]
-                p, q = spread(lefts[h0 + k], i), spread(rights[h0 + k], i)
-                for t in range(j):
-                    p = p - low[j][t] * u[t]
-                    q = q - low[j][t] * v[t]
-                u.append(p * r)
-                v.append(q * r)
-                u_rows[k] = jnp.where(sub == i, u[j], u_rows[k])
-                v_rows[k] = jnp.where(sub == i, v[j], v_rows[k])
-            us += u_rows
-            vs += v_rows
-            for h in range(h0 + K, H):
-                for j in range(BLK):
-                    lefts[h] = lefts[h] - cols[j][h] * u[j]
-                    rights[h] = rights[h] - cols[j][h] * v[j]
+                        cols[c][h] = cols[c][h] - cols[j][h] * scaled
+                for h in range(k if i < SUB - 1 else k + 1, H):
+                    lefts[h] = lefts[h] - cols[j][h] * u
+                    rights[h] = rights[h] - cols[j][h] * v
         u_all = jnp.concatenate(us, axis=0)
         v_all = jnp.concatenate(vs, axis=0)
         t_ref[pl.ds(start, G), :] = v_all
+        if isinstance(g, int):
+            for stage in hooks[g]:
+                stage()
+            return carry
         both = jnp.concatenate([u_all, v_all], axis=1)
         high = both.astype(BF16).astype(F32)
         low = both - high
         lhs = jnp.concatenate([high[:, :TILE], high[:, :TILE], low[:, :TILE]], axis=0)
         rhs = jnp.concatenate([high, low, high], axis=0)
         d_ref[...] -= dot(lhs.astype(BF16), rhs.astype(BF16), ((0,), (0,)))
-        for k, stages in enumerate(hooks):
+        for k, stages in enumerate(hooks[:-1]):
             if stages:
                 @pl.when(g == k)
                 def _():
@@ -288,12 +285,13 @@
                         stage()
         return carry
 
-    lax.fori_loop(0, TILE // G, step, 0)
+    lax.fori_loop(0, TILE // G - 1, step, 0)
+    step(TILE // G - 1, 0)
 
 
 def ace_kernel(bands, groups, orb, kern, blk, ace, exch, full, extra, w, wx, a, rest, x16, xlow, mba,
-               d_ref, t_ref, proj, proj2, bfull, acc, applied, loc, m_s, m_r, n_s, n_r, c_s, c_r,
-               d_s, d_r, b_s, b_r, p_s, p_r, t_s, t_r, e_s, e_r, *scratch):
+               d_ref, t_ref, proj, proj2, bfull, acc, applied, applied2, back, loc, m_s, m_r, n_s, n_r, c_s, c_r,
+               d_s, d_r, b_s, b_r, p_s, p_r, t_s, t_r, e_s, e_r, f_s, f_r, *scratch):
     at = Place(bands, groups)
     me, team = at.me, at.team
     own, bown = ace.shape[0], exch.shape[0]
@@ -332,25 +330,39 @@
         p = at.rival(t)
         return remote(orb.at[:, chunk(p)], mine, c_s.at[t], c_r.at[sender], {"band": p})
 
-    def twin_rival(t, sender, lo=0, size=own):
+    parts = [(0, cols // 2 // LANES * LANES), (cols // 2 // LANES * LANES, cols)]
+    parts = [part for part in parts if part[0] < part[1]]
+
+    def twin_rival(t, sender, lo, hi):
         p = at.rival(t)
-        return remote(orb.at[pl.ds(lo, size), twin(p)], extra.at[span(me, size, lo, own)],
-                      d_s.at[t], d_r.at[sender], {"band": p})
-
-    slices = [(t, lo) for lo in range(0, own, SLICE) for t in range(team)]
-
-    def upward(count):
+        first = pl.multiple_of(lax.rem(p + team, bands) * cols + lo, TILE)
+        k = 0 if hi <= parts[0][1] else 1
+        return remote(orb.at[:, pl.ds(first, hi - lo)], extra.at[span(me, own), lo:hi],
+                      d_s.at[t, k], d_r.at[sender, k], {"band": p})
+
+    slices = [(t, lo) for lo in range(0, cols, LANES) for t in range(team)]
+    left = {True: list(slices), False: list(slices)}
+    near = at.rank >= team // 2
+
+    def upward(count, first=True):
+        batch, left[first][:] = left[first][:count], left[first][count:]
+
         def go():
-            @pl.when(at.half == 0)
+            @pl.when((at.half == 0) & (near if first else ~near))
             def _():
                 for t, lo in batch:
-                    twin_rival(t, at.rank, lo, SLICE).start()
-        batch, slices[:] = slices[:count], slices[count:]
+                    twin_rival(t, at.rank, lo, lo + LANES).start()
         return go
 
-    def blocks():
-        return [remote(blk.at[:, chunk(at.peer[d])], bmine, b_s.at[d], b_r.at[d], at.band(d))
-                for d in at.far]
+    def block(slot, p, sender):
+        return remote(blk.at[:, chunk(p)], bmine, b_s.at[slot], b_r.at[sender], {"band": p})
+
+    def block_rival(t):
+        return lambda: block(t, at.rival(t), me).start()
+
+    def block_mates():
+        for j in range(1, team):
+            block(team + j, at.half * team + at.mate(j), me).start()
 
     def bkept():
         return pltpu.make_async_copy(blk.at[:, chunk(me)], bmine, loc.at[2])
@@ -398,10 +410,13 @@
             row += TILE
     cross.pad(row)
     cross.s1()
+    for t in range(team - 1):
+        block_rival(t)()
+    cross.s2()
     inner.s5()
-    for copy in blocks():
-        copy.start()
-    cross.s2()
+    cross.s3()
+    block_rival(team - 1)()
+    block_mates()
     inner.s6()
     inner.s7()
     row = 0
@@ -417,8 +432,8 @@
 
     def couple_start():
         bkept().wait()
-        for copy in blocks():
-            copy.wait()
+        for d in range(1, bands):
+            block(d, at.peer[d], at.peer[d]).wait_recv()
         half = nblk // 2
         for h in range(2):
             couple.put(h * n, dot(w[...], bfull[h * half:(h + 1) * half, :], ((1,), (1,))))
@@ -429,16 +444,31 @@
 
     def piece(q, r0, r1, source, target, other):
         lo = r0 % own
-        rows, sent, got = (proj2, t_s, t_r) if other else (proj, p_s, p_r)
-        where = twin(source) if other else chunk(source)
-        return remote(rows.at[r0:r1], ace.at[lo:lo + r1 - r0, where],
-                      sent.at[q], got.at[q, source], {"band": target})
+        if other:
+            return strip(q, r0, r1, source, target, 0, 0, cols)
+        return remote(proj.at[r0:r1], ace.at[lo:lo + r1 - r0, chunk(source)],
+                      p_s.at[q], p_r.at[q, source], {"band": target})
 
     def stay(q, r0, r1, other):
         lo = r0 % own
-        rows, sent = (proj2, t_s) if other else (proj, p_s)
-        where = twin(me) if other else chunk(me)
-        return pltpu.make_async_copy(rows.at[r0:r1], ace.at[lo:lo + r1 - r0, where], sent.at[q])
+        if other:
+            return strip_stay(q, r0, r1, 0, 0, cols)
+        return pltpu.make_async_copy(
+            proj.at[r0:r1], ace.at[lo:lo + r1 - r0, chunk(me)], p_s.at[q])
+
+    def some(source, c0, c1):
+        first = lax.rem(source + team, bands) * cols + c0
+        return pl.ds(pl.multiple_of(first, TILE), c1 - c0)
+
+    def strip(q, r0, r1, source, target, k, c0, c1):
+        lo = r0 % own
+        return remote(proj2.at[r0:r1, c0:c1], ace.at[lo:lo + r1 - r0, some(source, c0, c1)],
+                      t_s.at[q, k], t_r.at[q, source, k], {"band": target})
+
+    def strip_stay(q, r0, r1, k, c0, c1):
+        lo = r0 % own
+        return pltpu.make_async_copy(
+            proj2.at[r0:r1, c0:c1], ace.at[lo:lo + r1 - r0, some(me, c0, c1)], t_s.at[q, k])
 
     def deliver(lo, hi, other):
         for q, (r0, r1) in pieces:
@@ -453,24 +483,16 @@
                 def _():
                     stay(q, r0, r1, other).start()
 
-    def project(lo, hi):
-        proj2[lo:hi, :] = (dot(x16[lo:hi, 0:hi], wx[0:hi, :], ((1,), (0,)))
-                           + dot(xlow[lo:hi, 0:hi], wx[0:hi, :], ((1,), (0,)))).astype(BF16)
+    def project(lo, hi, c0, c1):
+        proj2[lo:hi, c0:c1] = (dot(x16[lo:hi, 0:hi], wx[0:hi, c0:c1], ((1,), (0,)))
+                               + dot(xlow[lo:hi, 0:hi], wx[0:hi, c0:c1], ((1,), (0,)))).astype(BF16)
 
     def spare():
         @pl.when(at.half == 0)
         def _():
-            project(0, n2)
-
-        for other in (0, 1):
-            deliver(0, n2, other)
-
-    def arrive():
-        @pl.when(at.half == 1)
-        def _():
-            for t in range(team):
-                twin_rival(t, t).wait_recv()
-            wx[0:n2, :] = weigh(extra[0:n2, :], twin(me))
+            project(0, n2, 0, cols)
+
+        deliver(0, n2, 1)
 
     tiles = n2 // TILE
     hooks = [[[] for _ in range(4)] for _ in range(2 * tiles)]
@@ -478,20 +500,17 @@
     def at_hook(k, g, *stages):
         hooks[k][g] += stages
 
-    for g in range(4):
-        at_hook(0, g, upward(1))
-        at_hook(tiles - 2, g, upward(1))
-        at_hook(tiles - 1, g, upward(1))
-    at_hook(0, 1, cross.s3)
+    at_hook(0, 2, cross.s4)
     at_hook(tiles - 2, 0, couple_start)
-    at_hook(tiles - 2, 1, cross.s4)
-    at_hook(tiles - 2, 3, couple.s2)
-    at_hook(tiles - 1, 0, cross.s5)
-    at_hook(tiles - 1, 1, couple.s3)
-    at_hook(tiles - 1, 2, cross.s6)
-    at_hook(tiles, 1, couple.s5, upward(len(slices)), spare)
-    at_hook(tiles, 3, couple.s6)
-    at_hook(tiles + 1, 0, couple.s7)
+    at_hook(tiles - 2, 2, couple.s2)
+    at_hook(tiles - 2, 3, cross.s5, upward(1), upward(1, False))
+    at_hook(tiles - 1, 0, upward(1), upward(1, False))
+    at_hook(tiles - 1, 1, upward(1))
+    at_hook(tiles - 1, 3, couple.s3, cross.s6)
+    at_hook(tiles, 0, upward(len(slices)))
+    at_hook(tiles + 1, 1, couple.s5, upward(len(slices), False), spare)
+    at_hook(tiles + 2, 1, couple.s6)
+    at_hook(tiles + 2, 3, couple.s7)
 
     def attach(lo, hi):
         half = nblk // 2
@@ -542,49 +561,119 @@
                     dot(bh[c:], bh[c:d], both) + (dot(bh[c:], bl[c:d], both) + dot(bl[c:], bh[c:d], both)))
             over = ((1,), (0,))
             xh = x16[0:n2, 0:n2]
+            couple.s4()
+            deliver(0, n2, 0)
             rest[n2:, 0:n2] = -(dot(bh, xh, over) + (dot(bh, xlow[0:n2, 0:n2], over) + dot(bl, xh, over)))
-            couple.s4()
-        if e == n - TILE:
-            attach(0, e)
-    attach(n - TILE, n)
+    attach(0, n)
     applied[...] = (-acc[...]).astype(BF16)
-    outs = [remote(applied.at[span(at.peer[d], bown)], exch.at[:, chunk(me)],
-                   e_s.at[d], e_r.at[d], at.band(d)) for d in at.far]
-    outs.append(pltpu.make_async_copy(applied.at[span(me, bown)], exch.at[:, chunk(me)], loc.at[3]))
-    for copy in outs:
-        copy.start()
-    arrive()
+
+    def out(slot, p, sender):
+        return remote(applied.at[span(p, bown)], exch.at[:, chunk(sender)],
+                      e_s.at[slot], e_r.at[sender], {"band": p})
+
+    def out2(slot, p, sender):
+        return remote(applied2.at[span(lax.rem(p, team), bown)], exch.at[:, twin(sender)],
+                      f_s.at[slot], f_r.at[sender], {"band": p})
+
+    def held():
+        return pltpu.make_async_copy(applied.at[span(me, bown)], exch.at[:, chunk(me)], loc.at[3])
+
+    def held2():
+        return pltpu.make_async_copy(applied2.at[span(at.rank, bown)], exch.at[:, twin(me)], loc.at[4])
+
+    mates = [at.half * team + at.mate(j) for j in range(1, team)]
 
     @pl.when(at.half == 1)
     def _():
-        project(n2, n)
-
-    deliver(n2, n, 1)
+        for t in range(team):
+            out(t, at.rival(t), me).start()
+
+    for j, p in enumerate(mates):
+        out(team + j, p, me).start()
+    held().start()
+
+    @pl.when(at.half == 1)
+    def _():
+        turned = ((0,), (0,))
+        part = dot(x16[...], couple.allg[n:2 * n, :], ((1,), (0,))) * -scale
+        ph, pq = split(part)
+        back[...] = (dot(ph, x16[...], turned)
+                     + (dot(ph, xlow[...], turned) + dot(pq, x16[...], turned)))
+
+    @pl.when(at.half == 1)
+    def _():
+        bh, bl = split(back[...])
+        forth = ((1,), (0,))
+        for k, (c0, c1) in enumerate(parts):
+            for t in range(team):
+                twin_rival(t, t, c0, c1).wait_recv()
+            wx[0:n2, c0:c1] = (-(extra[0:n2, c0:c1].astype(F32) * kern[:, some(me, c0, c1)])).astype(BF16)
+            project(n2, n, c0, c1)
+            for q, (r0, r1) in pieces:
+                if r0 >= n2:
+                    owner = r0 // own
+
+                    @pl.when(me != owner)
+                    def _():
+                        strip(q, r0, r1, me, owner, k, c0, c1).start()
+
+                    @pl.when(me == owner)
+                    def _():
+                        strip_stay(q, r0, r1, k, c0, c1).start()
+
+            applied2[:, c0:c1] = (dot(bh, wx[:, c0:c1], forth) + dot(bl, wx[:, c0:c1], forth)).astype(BF16)
+        for j, p in enumerate(mates):
+            out2(j, p, me).start()
+        held2().start()
+
     for t in range(team):
         to_rival(t, t).wait_send()
+        block(t, me, me).wait_send()
+    for j in range(1, team):
+        block(team + j, me, me).wait_send()
 
     @pl.when(at.half == 0)
     def _():
         for t in range(team):
-            twin_rival(t, t).wait_send()
+            for c0, c1 in parts:
+                twin_rival(t, t, c0, c1).wait_send()
 
     for q, (r0, r1) in pieces:
         owner = r0 // own
+        cells = list(enumerate(parts)) if r0 >= n2 else [(0, (0, cols))]
 
         @pl.when((me != owner) & (at.half == owner // team))
         def _():
-            for other in (0, 1):
-                piece(q, r0, r1, me, owner, other).wait_send()
+            piece(q, r0, r1, me, owner, 0).wait_send()
+            for k, (c0, c1) in cells:
+                strip(q, r0, r1, me, owner, k, c0, c1).wait_send()
 
         @pl.when(me == owner)
         def _():
-            for other in (0, 1):
-                stay(q, r0, r1, other).wait()
-                for j in range(1, team):
-                    mate = at.half * team + at.mate(j)
-                    piece(q, r0, r1, mate, mate, other).wait_recv()
-    for copy in outs:
-        copy.wait()
+            stay(q, r0, r1, 0).wait()
+            for k, (c0, c1) in cells:
+                strip_stay(q, r0, r1, k, c0, c1).wait()
+            for mate in mates:
+                piece(q, r0, r1, mate, mate, 0).wait_recv()
+                for k, (c0, c1) in cells:
+                    strip(q, r0, r1, mate, mate, k, c0, c1).wait_recv()
+
+    for j, p in enumerate(mates):
+        out(team + j, p, p).wait()
+    held().wait()
+
+    @pl.when(at.half == 1)
+    def _():
+        for t in range(team):
+            out(t, at.rival(t), me).wait_send()
+        for j, p in enumerate(mates):
+            out2(j, p, p).wait()
+        held2().wait()
+
+    @pl.when(at.half == 0)
+    def _():
+        for t in range(team):
+            out(t, me, at.rival(t)).wait_recv()
 
 
 def shards(orbitals, kernel, block_vectors):
@@ -631,9 +720,11 @@
             pltpu.VMEM((nblk, cols), BF16),
             pltpu.VMEM((nblk, cols), F32),
             pltpu.VMEM((nblk, cols), BF16),
-            dma((4,)), some, some, some, some, some, some, some, some,
-            many, many, dma((pieces,)), dma((pieces, bands)), dma((pieces,)), dma((pieces, bands)),
-            many, many,
+            pltpu.VMEM((nblk // 2, cols), BF16),
+            pltpu.VMEM((nblk // 2, n), F32),
+            dma((5,)), some, some, some, some, some, some, dma((team, 2)), dma((team, 2)),
+            many, many, dma((pieces,)), dma((pieces, bands)), dma((pieces, 2)), dma((pieces, bands, 2)),
+            many, many, many, many,
         ]
         + reduce_scratch(padded(tiles * (tiles + 1) // 2 * TILE, team), team, bands, levels, 2)
         + reduce_scratch(padded(tiles * tiles * TILE, bands), bands, bands, levels, 1)

time: 105 us -> 99.3 us (0.946)
  Pallas kernels: 100 us -> 94.3 us
    pallas_call x1, Pallas kernels: 100 us -> 94.3 us  [shards(): pl.pallas_call(functools.partial(ace_kernel, bands, groups), name='ace',...]
where the time goes in v3:
time: 99.3 us; the launch traced here: 98.1 us
  Pallas kernels  94.3 us (95%)
  local copies, waits for them, and re-layouts  3.16 us (3%)
    pallas_call x1, Pallas kernels, shards(): pl.pallas_call(functools.partial(ace_kernel, bands, groups), name='ace',...  94.3 us
    unnamed x4, local copies, waits for them, and re-layouts  3.16 us

profile of v3, /device:TPU:18, one launch (start us, length us, event | category | flops | bytes accessed | tf_op | source)
XLA Modules:
  0.0 98.1 jit_solution(10452241306721960790)
XLA Ops:
  0.6 94.3 %ace.1 = (bf16[192,3072]{1,0:T(8,128)(2,1)}, bf16[64,3072]{1,0:T(8,128)(2,1)}) custom-call(bf16[192,3072]{1,0:T(8,128)(2,1)} %orb.1, f32[1,3072]{1,0:T(1,128)} %bitcast.1, bf16[64,3072]{1,0:T(8,128)(2,1)} %blk.1), custom_call_target="tpu_custom_call" | custom-call | tf_op jit(solution)/shard_map/ace/pallas_call | solution.py:697
  94.9 0.0 copy-start
  94.9 2.4 %copy.7 = bf16[192,3072]{1,0:T(8,128)(2,1)} copy(bf16[192,3072]{1,0:T(8,128)(2,1)} %get-tuple-element.4) | data formatting | bytes 2359296
  97.3 0.0 copy-done
  97.3 0.7 copy.8
Async XLA Ops:
  94.9 2.4 %copy-start = (bf16[64,3072]{1,0:T(8,128)(2,1)S(1)}, bf16[64,3072]{1,0:T(8,128)(2,1)}, u32[]{:S(2)}) copy-start(bf16[64,3072]{1,0:T(8,128)(2,1)} %get-tuple-element.5) | copy-start | bytes 1179652

commit v4 on v3

--- a/solution.py
+++ b/solution.py
@@ -81,9 +81,9 @@
         ((levels, h3, TILE), BF16), ((levels, h3, TILE), BF16), ((sides * rows, TILE), BF16),
     ]
     return [pltpu.VMEM(*shape) for shape in shapes] + [
-        dma((4,)), dma((parts,)), dma((parts,)), dma((levels,)), dma((levels,)),
+        dma((4,)), dma((1,)), dma((1,)), dma((levels,)), dma((levels,)),
         dma((bands,)), dma((bands,)), dma((bands,)), dma((bands,)),
-        dma((2 * bands,)), dma((2 * bands,)),
+        dma((1,)), dma((1,)),
     ]
 
 
@@ -129,7 +129,7 @@
 
     def to_parts(self):
         return [remote(self.b16.at[span(index, self.h3)], self.rx3.at[slot],
-                       self.z_s.at[slot], self.z_r.at[slot], where)
+                       self.z_s.at[0], self.z_r.at[0], where)
                 for slot, index, where in self.parts]
 
     def piece(self, d, row):
@@ -152,8 +152,7 @@
     def last(self, d, other):
         row = 1 - self.at.row if other else self.at.row
         there = self.allg.at[self.piece(d, row)]
-        e = d + self.at.bands * other
-        return remote(there, there, self.f_s.at[e], self.f_r.at[e], self.at.partner)
+        return remote(there, there, self.f_s.at[0], self.f_r.at[0], self.at.partner)
 
     def s1(self):
         self.to_partner().start()
@@ -173,8 +172,8 @@
 
     def s4(self):
         at = self.at
-        for copy in self.to_parts():
-            copy.wait()
+        whole = self.rx3.at[0:len(self.parts)]
+        remote(whole, whole, self.z_s.at[0], self.z_r.at[0], self.parts[0][2]).wait()
         total = self.b32[span(self.mine, self.h3), :]
         for slot, _, _ in self.parts:
             total = total + self.rx3[slot].astype(F32)
@@ -202,9 +201,8 @@
             self.last(d, 1).start()
 
     def s7(self):
-        for d in [0] + self.at.near:
-            self.last(d, 0).wait()
-            self.last(d, 1).wait()
+        whole = self.allg.at[0:2 * self.at.bands * self.h3]
+        remote(whole, whole, self.f_s.at[0], self.f_r.at[0], self.at.partner).wait()
 
 
 def split(a):
@@ -291,7 +289,7 @@
 
 def ace_kernel(bands, groups, orb, kern, blk, ace, exch, full, extra, w, wx, a, rest, x16, xlow, mba,
                d_ref, t_ref, proj, proj2, bfull, acc, applied, applied2, back, loc, m_s, m_r, n_s, n_r, c_s, c_r,
-               d_s, d_r, b_s, b_r, p_s, p_r, t_s, t_r, e_s, e_r, f_s, f_r, *scratch):
+               d_s, d_r, b_s, b_r, p_s, p_r, t_s, e_s, e_r, f_s, f_r, *scratch):
     at = Place(bands, groups)
     me, team = at.me, at.team
     own, bown = ace.shape[0], exch.shape[0]
@@ -340,7 +338,7 @@
         return remote(orb.at[:, pl.ds(first, hi - lo)], extra.at[span(me, own), lo:hi],
                       d_s.at[t, k], d_r.at[sender, k], {"band": p})
 
-    slices = [(t, lo) for lo in range(0, cols, LANES) for t in range(team)]
+    slices = [(t, lo) for t in reversed(range(team)) for lo in range(0, cols, LANES)]
     left = {True: list(slices), False: list(slices)}
     near = at.rank >= team // 2
 
@@ -447,14 +445,14 @@
         if other:
             return strip(q, r0, r1, source, target, 0, 0, cols)
         return remote(proj.at[r0:r1], ace.at[lo:lo + r1 - r0, chunk(source)],
-                      p_s.at[q], p_r.at[q, source], {"band": target})
+                      p_s.at[0], p_r.at[0], {"band": target})
 
     def stay(q, r0, r1, other):
         lo = r0 % own
         if other:
             return strip_stay(q, r0, r1, 0, 0, cols)
         return pltpu.make_async_copy(
-            proj.at[r0:r1], ace.at[lo:lo + r1 - r0, chunk(me)], p_s.at[q])
+            proj.at[r0:r1], ace.at[lo:lo + r1 - r0, chunk(me)], t_s.at[0])
 
     def some(source, c0, c1):
         first = lax.rem(source + team, bands) * cols + c0
@@ -463,12 +461,12 @@
     def strip(q, r0, r1, source, target, k, c0, c1):
         lo = r0 % own
         return remote(proj2.at[r0:r1, c0:c1], ace.at[lo:lo + r1 - r0, some(source, c0, c1)],
-                      t_s.at[q, k], t_r.at[q, source, k], {"band": target})
+                      p_s.at[0], p_r.at[0], {"band": target})
 
     def strip_stay(q, r0, r1, k, c0, c1):
         lo = r0 % own
         return pltpu.make_async_copy(
-            proj2.at[r0:r1, c0:c1], ace.at[lo:lo + r1 - r0, some(me, c0, c1)], t_s.at[q, k])
+            proj2.at[r0:r1, c0:c1], ace.at[lo:lo + r1 - r0, some(me, c0, c1)], t_s.at[0])
 
     def deliver(lo, hi, other):
         for q, (r0, r1) in pieces:
@@ -502,13 +500,15 @@
 
     at_hook(0, 2, cross.s4)
     at_hook(tiles - 2, 0, couple_start)
-    at_hook(tiles - 2, 2, couple.s2)
-    at_hook(tiles - 2, 3, cross.s5, upward(1), upward(1, False))
+    at_hook(tiles - 2, 2, cross.s5, couple.s2)
+    at_hook(tiles - 2, 3, upward(1), upward(1, False))
     at_hook(tiles - 1, 0, upward(1), upward(1, False))
     at_hook(tiles - 1, 1, upward(1))
-    at_hook(tiles - 1, 3, couple.s3, cross.s6)
-    at_hook(tiles, 0, upward(len(slices)))
-    at_hook(tiles + 1, 1, couple.s5, upward(len(slices), False), spare)
+    at_hook(tiles - 1, 2, cross.s6)
+    closing = upward(3)
+    at_hook(tiles, 1, couple.s4, lambda: deliver(0, n2, 0), upward(len(slices)))
+    at_hook(tiles + 1, 0, upward(len(slices), False))
+    at_hook(tiles + 1, 2, couple.s5, spare)
     at_hook(tiles + 2, 1, couple.s6)
     at_hook(tiles + 2, 3, couple.s7)
 
@@ -561,8 +561,8 @@
                     dot(bh[c:], bh[c:d], both) + (dot(bh[c:], bl[c:d], both) + dot(bl[c:], bh[c:d], both)))
             over = ((1,), (0,))
             xh = x16[0:n2, 0:n2]
-            couple.s4()
-            deliver(0, n2, 0)
+            couple.s3()
+            closing()
             rest[n2:, 0:n2] = -(dot(bh, xh, over) + (dot(bh, xlow[0:n2, 0:n2], over) + dot(bl, xh, over)))
     attach(0, n)
     applied[...] = (-acc[...]).astype(BF16)
@@ -638,26 +638,10 @@
             for c0, c1 in parts:
                 twin_rival(t, t, c0, c1).wait_send()
 
-    for q, (r0, r1) in pieces:
-        owner = r0 // own
-        cells = list(enumerate(parts)) if r0 >= n2 else [(0, (0, cols))]
-
-        @pl.when((me != owner) & (at.half == owner // team))
-        def _():
-            piece(q, r0, r1, me, owner, 0).wait_send()
-            for k, (c0, c1) in cells:
-                strip(q, r0, r1, me, owner, k, c0, c1).wait_send()
-
-        @pl.when(me == owner)
-        def _():
-            stay(q, r0, r1, 0).wait()
-            for k, (c0, c1) in cells:
-                strip_stay(q, r0, r1, k, c0, c1).wait()
-            for mate in mates:
-                piece(q, r0, r1, mate, mate, 0).wait_recv()
-                for k, (c0, c1) in cells:
-                    strip(q, r0, r1, mate, mate, k, c0, c1).wait_recv()
-
+    everything = ace.at[:, 0:2 * cols * (team - 1)]
+    remote(everything, everything, p_s.at[0], p_r.at[0], {"band": mates[0]}).wait()
+    local = ace.at[:, 0:2 * cols]
+    pltpu.make_async_copy(local, local, t_s.at[0]).wait()
     for j, p in enumerate(mates):
         out(team + j, p, p).wait()
     held().wait()
@@ -690,7 +674,6 @@
         unit = 4 * parts * 16
         return -(-rows // unit) * unit
 
-    pieces = len(set(range(0, n, TILE)) | set(range(0, n, own)))
     vmem, hbm = pl.BlockSpec(memory_space=pltpu.VMEM), pl.BlockSpec(memory_space=pl.ANY)
     dma = pltpu.SemaphoreType.DMA
     many, some = dma((bands,)), dma((team,))
@@ -723,7 +706,7 @@
             pltpu.VMEM((nblk // 2, cols), BF16),
             pltpu.VMEM((nblk // 2, n), F32),
             dma((5,)), some, some, some, some, some, some, dma((team, 2)), dma((team, 2)),
-            many, many, dma((pieces,)), dma((pieces, bands)), dma((pieces, 2)), dma((pieces, bands, 2)),
+            many, many, dma((1,)), dma((1,)), dma((1,)),
             many, many, many, many,
         ]
         + reduce_scratch(padded(tiles * (tiles + 1) // 2 * TILE, team), team, bands, levels, 2)

time: 99.3 us -> 95.4 us (0.961); the launches traced: 98.1 us -> 95.2 us
  Pallas kernels: 94.3 us -> 91.4 us
    pallas_call x1, Pallas kernels: 94.3 us -> 91.4 us  [shards(): pl.pallas_call(functools.partial(ace_kernel, bands, groups), name='ace',...]
where the time goes in v4:
time: 95.4 us; the launch traced here: 95.2 us
  Pallas kernels  91.4 us (96%)
  local copies, waits for them, and re-layouts  3.16 us (3%)
    pallas_call x1, Pallas kernels, shards(): pl.pallas_call(functools.partial(ace_kernel, bands, groups), name='ace',...  91.4 us
    unnamed x4, local copies, waits for them, and re-layouts  3.16 us

profile of v4, /device:TPU:18, one launch (start us, length us, event | category | flops | bytes accessed | tf_op | source)
XLA Modules:
  0.0 95.2 jit_solution(7610591984332249877)
XLA Ops:
  0.6 91.4 %ace.1 = (bf16[192,3072]{1,0:T(8,128)(2,1)}, bf16[64,3072]{1,0:T(8,128)(2,1)}) custom-call(bf16[192,3072]{1,0:T(8,128)(2,1)} %orb.1, f32[1,3072]{1,0:T(1,128)} %bitcast.1, bf16[64,3072]{1,0:T(8,128)(2,1)} %blk.1), custom_call_target="tpu_custom_call" | custom-call | tf_op jit(solution)/shard_map/ace/pallas_call | solution.py:680
  92.0 0.0 copy-start
  92.0 2.4 %copy.7 = bf16[192,3072]{1,0:T(8,128)(2,1)} copy(bf16[192,3072]{1,0:T(8,128)(2,1)} %get-tuple-element.4) | data formatting | bytes 2359296
  94.4 0.0 copy-done
  94.4 0.7 copy.8
Async XLA Ops:
  92.0 2.4 %copy-start = (bf16[64,3072]{1,0:T(8,128)(2,1)S(1)}, bf16[64,3072]{1,0:T(8,128)(2,1)}, u32[]{:S(2)}) copy-start(bf16[64,3072]{1,0:T(8,128)(2,1)} %get-tuple-element.5) | copy-start | bytes 1179652

commit v5 on v4

--- a/solution.py
+++ b/solution.py
@@ -82,7 +82,7 @@
     ]
     return [pltpu.VMEM(*shape) for shape in shapes] + [
         dma((4,)), dma((1,)), dma((1,)), dma((levels,)), dma((levels,)),
-        dma((bands,)), dma((bands,)), dma((bands,)), dma((bands,)),
+        dma((bands,)), dma((bands,)), dma((1,)), dma((1,)),
         dma((1,)), dma((1,)),
     ]
 
@@ -147,7 +147,7 @@
 
     def side(self, d):
         there = self.allg.at[self.piece(d, self.at.row)]
-        return remote(there, there, self.y_s.at[d], self.y_r.at[d], self.at.across)
+        return remote(there, there, self.y_s.at[0], self.y_r.at[0], self.at.across)
 
     def last(self, d, other):
         row = 1 - self.at.row if other else self.at.row
@@ -196,8 +196,9 @@
             self.last(d, 0).start()
 
     def s6(self):
+        whole = self.allg.at[0:self.at.bands * self.h3]
+        remote(whole, whole, self.y_s.at[0], self.y_r.at[0], self.at.across).wait()
         for d in [0] + self.at.near:
-            self.side(d).wait()
             self.last(d, 1).start()
 
     def s7(self):
@@ -287,7 +288,7 @@
     step(TILE // G - 1, 0)
 
 
-def ace_kernel(bands, groups, orb, kern, blk, ace, exch, full, extra, w, wx, a, rest, x16, xlow, mba,
+def ace_kernel(bands, groups, orb, kern_in, blk, ace, exch, kern, full, extra, w, wx, a, rest, x16, xlow, mba,
                d_ref, t_ref, proj, proj2, bfull, acc, applied, applied2, back, loc, m_s, m_r, n_s, n_r, c_s, c_r,
                d_s, d_r, b_s, b_r, p_s, p_r, t_s, e_s, e_r, f_s, f_r, *scratch):
     at = Place(bands, groups)
@@ -314,7 +315,8 @@
 
     def kept():
         return [pltpu.make_async_copy(orb.at[:, chunk(me)], mine, loc.at[0]),
-                pltpu.make_async_copy(orb.at[:, twin(me)], also, loc.at[1])]
+                pltpu.make_async_copy(orb.at[:, twin(me)], also, loc.at[1]),
+                pltpu.make_async_copy(kern_in, kern, loc.at[5])]
 
     def to_mates():
         copies = []
@@ -395,7 +397,6 @@
     inner.s1()
     inner.s2()
     inner.s3()
-    inner.s4()
     for t in range(team):
         to_rival(t, t).wait_recv()
     other = span(1 - at.half, n2)
@@ -408,6 +409,7 @@
             row += TILE
     cross.pad(row)
     cross.s1()
+    inner.s4()
     for t in range(team - 1):
         block_rival(t)()
     cross.s2()
@@ -498,13 +500,15 @@
     def at_hook(k, g, *stages):
         hooks[k][g] += stages
 
-    at_hook(0, 2, cross.s4)
+    at_hook(0, 1, cross.s4, upward(2))
+    at_hook(0, 3, upward(1))
     at_hook(tiles - 2, 0, couple_start)
-    at_hook(tiles - 2, 2, cross.s5, couple.s2)
+    at_hook(tiles - 2, 1, cross.s5)
+    at_hook(tiles - 2, 2, couple.s2)
     at_hook(tiles - 2, 3, upward(1), upward(1, False))
     at_hook(tiles - 1, 0, upward(1), upward(1, False))
     at_hook(tiles - 1, 1, upward(1))
-    at_hook(tiles - 1, 2, cross.s6)
+    at_hook(tiles - 1, 1, cross.s6)
     closing = upward(3)
     at_hook(tiles, 1, couple.s4, lambda: deliver(0, n2, 0), upward(len(slices)))
     at_hook(tiles + 1, 0, upward(len(slices), False))
@@ -674,7 +678,7 @@
         unit = 4 * parts * 16
         return -(-rows // unit) * unit
 
-    vmem, hbm = pl.BlockSpec(memory_space=pltpu.VMEM), pl.BlockSpec(memory_space=pl.ANY)
+    hbm = pl.BlockSpec(memory_space=pl.ANY)
     dma = pltpu.SemaphoreType.DMA
     many, some = dma((bands,)), dma((team,))
     return pl.pallas_call(
@@ -684,9 +688,10 @@
             jax.ShapeDtypeStruct((own, width), BF16),
             jax.ShapeDtypeStruct((bown, width), BF16),
         ),
-        in_specs=[hbm, vmem, hbm],
+        in_specs=[hbm, hbm, hbm],
         out_specs=(hbm, hbm),
         scratch_shapes=[
+            pltpu.VMEM((1, width), F32),
             pltpu.VMEM((n, cols), BF16),
             pltpu.VMEM((n, cols), BF16),
             pltpu.VMEM((n, cols), BF16),
@@ -705,7 +710,7 @@
             pltpu.VMEM((nblk, cols), BF16),
             pltpu.VMEM((nblk // 2, cols), BF16),
             pltpu.VMEM((nblk // 2, n), F32),
-            dma((5,)), some, some, some, some, some, some, dma((team, 2)), dma((team, 2)),
+            dma((6,)), some, some, some, some, some, some, dma((team, 2)), dma((team, 2)),
             many, many, dma((1,)), dma((1,)), dma((1,)),
             many, many, many, many,
         ]

time: 95.4 us -> 93.4 us (0.979)
  Pallas kernels: 91.4 us -> 89.4 us
    pallas_call x1, Pallas kernels: 91.4 us -> 89.4 us  [shards(): pl.pallas_call(functools.partial(ace_kernel, bands, groups), name='ace',...]
where the time goes in v5:
time: 93.4 us; the launch traced here: 93.2 us
  Pallas kernels  89.4 us (96%)
  local copies, waits for them, and re-layouts  3.16 us (3%)
    pallas_call x1, Pallas kernels, shards(): pl.pallas_call(functools.partial(ace_kernel, bands, groups), name='ace',...  89.4 us
    unnamed x4, local copies, waits for them, and re-layouts  3.16 us

profile of v5, /device:TPU:18, one launch (start us, length us, event | category | flops | bytes accessed | tf_op | source)
XLA Modules:
  0.0 93.2 jit_solution(13922848501243220469)
XLA Ops:
  0.6 89.4 %ace.1 = (bf16[192,3072]{1,0:T(8,128)(2,1)}, bf16[64,3072]{1,0:T(8,128)(2,1)}) custom-call(bf16[192,3072]{1,0:T(8,128)(2,1)} %orb.1, f32[1,3072]{1,0:T(1,128)} %bitcast.1, bf16[64,3072]{1,0:T(8,128)(2,1)} %blk.1), custom_call_target="tpu_custom_call" | custom-call | tf_op jit(solution)/shard_map/ace/pallas_call | solution.py:684
  90.1 0.0 copy-start
  90.1 2.4 %copy.7 = bf16[192,3072]{1,0:T(8,128)(2,1)} copy(bf16[192,3072]{1,0:T(8,128)(2,1)} %get-tuple-element.4) | data formatting | bytes 2359296
  92.5 0.0 copy-done
  92.5 0.7 copy.8
Async XLA Ops:
  90.1 2.4 %copy-start = (bf16[64,3072]{1,0:T(8,128)(2,1)S(1)}, bf16[64,3072]{1,0:T(8,128)(2,1)}, u32[]{:S(2)}) copy-start(bf16[64,3072]{1,0:T(8,128)(2,1)} %get-tuple-element.5) | copy-start | bytes 1179652

commit v6 on v5

--- a/solution.py
+++ b/solution.py
@@ -510,8 +510,8 @@
     at_hook(tiles - 1, 1, upward(1))
     at_hook(tiles - 1, 1, cross.s6)
     closing = upward(3)
-    at_hook(tiles, 1, couple.s4, lambda: deliver(0, n2, 0), upward(len(slices)))
-    at_hook(tiles + 1, 0, upward(len(slices), False))
+    at_hook(tiles, 1, couple.s4, lambda: deliver(0, n2 - TILE, 0), upward(len(slices)))
+    at_hook(tiles + 1, 0, upward(len(slices), False), lambda: deliver(n2 - TILE, n2, 0))
     at_hook(tiles + 1, 2, couple.s5, spare)
     at_hook(tiles + 2, 1, couple.s6)
     at_hook(tiles + 2, 3, couple.s7)

time: 93.4 us -> 93 us (level)
  no operation moved by 1% of the time
where the time goes in v6:
time: 93 us; the launch traced here: 92.8 us
  Pallas kernels  89 us (96%)
  local copies, waits for them, and re-layouts  3.16 us (3%)
    pallas_call x1, Pallas kernels, shards(): pl.pallas_call(functools.partial(ace_kernel, bands, groups), name='ace',...  89 us
    unnamed x4, local copies, waits for them, and re-layouts  3.16 us

profile of v6, /device:TPU:18, one launch (start us, length us, event | category | flops | bytes accessed | tf_op | source)
XLA Modules:
  0.0 92.8 jit_solution(11374528851391124652)
XLA Ops:
  0.6 89.0 %ace.1 = (bf16[192,3072]{1,0:T(8,128)(2,1)}, bf16[64,3072]{1,0:T(8,128)(2,1)}) custom-call(bf16[192,3072]{1,0:T(8,128)(2,1)} %orb.1, f32[1,3072]{1,0:T(1,128)} %bitcast.1, bf16[64,3072]{1,0:T(8,128)(2,1)} %blk.1), custom_call_target="tpu_custom_call" | custom-call | tf_op jit(solution)/shard_map/ace/pallas_call | solution.py:684
  89.6 0.0 copy-start
  89.6 2.4 %copy.7 = bf16[192,3072]{1,0:T(8,128)(2,1)} copy(bf16[192,3072]{1,0:T(8,128)(2,1)} %get-tuple-element.4) | data formatting | bytes 2359296
  92.0 0.0 copy-done
  92.0 0.7 copy.8
Async XLA Ops:
  89.6 2.4 %copy-start = (bf16[64,3072]{1,0:T(8,128)(2,1)S(1)}, bf16[64,3072]{1,0:T(8,128)(2,1)}, u32[]{:S(2)}) copy-start(bf16[64,3072]{1,0:T(8,128)(2,1)} %get-tuple-element.5) | copy-start | bytes 1179652
